TPU v7x, 32 devices: a whole 2x2x4 slice. The times are simulated.
32 devices in a mesh: ctx: 8 (over z, y), head: 4 (over x, core).
Axes of the slice: x: 2, y: 2, z: 4, core: 2. Of those that a mesh axis runs over, the one named last changes fastest.
Arguments:
- queries: bfloat16 [1024, 8192], P('ctx', 'head'), may hold values from -6 to 6
- key_rows: bfloat16 [1024, 1024], P(('ctx', 'head')), may hold values from -6 to 6
- value_matrix_rows: bfloat16 [1024, 1024], P(('ctx', 'head')), may hold values from -6 to 6
- grad_out: bfloat16 [1024, 8192], P('ctx', 'head'), may hold values from -6 to 6
- doc_ids: int32 [1024], replicated, may hold values from 0 to 3, never falling along the last dimension, each value on 1 to 512 neighbouring positions
- block_owner: int32 [8, 8], replicated, may hold values from 0 to 7, each once within a row
Outputs:
- attention: bfloat16 [1024, 8192], P('ctx', 'head')
- owned_lse: float32 [64, 1024], P('head', 'ctx')
- grad_query: bfloat16 [1024, 8192], P('ctx', 'head')
- key_gradient: bfloat16 [1024, 1024], P(('ctx', 'head'))
- value_gradient: bfloat16 [1024, 1024], P(('ctx', 'head'))
Inputs may be any that keep to these rules, and one draw needn't show every extreme that they name: `doc_ids`: never falls along the tokens; every document holds 1 to 512 tokens. `block_owner`: entry [d, i] names the device that owns block i (tokens d * 128 + i * 16 onward, 16 of them) of token shard d; each row names every device once.
All inputs are finite; a program needn't handle non-finite values.
Results may differ from a plain program's by a relative error of at most 0.02.
Values may be sent and summed in bfloat16 or wider, within the bound.
No kernel may reach another device: no remote copies, remote signals or barrier semaphores. Data moves between devices by JAX's collectives and lax.ppermute only.
A program may use at most 64 MiB of HBM per device.

v0:
```python
import functools

import jax
import jax.numpy as jnp
from jax import lax
from jax.experimental import pallas as pl
from jax.experimental.pallas import tpu as pltpu
from jax.sharding import Mesh
from jax.sharding import PartitionSpec as P

HEAD_SIZE = 128
MASK = -1e30
LOG2E = 1.4426950408889634
LN2 = 0.6931471805599453
NT = (((1,), (1,)), ((), ()))
NN = (((1,), (0,)), ((), ()))
CTX = ("half", "sub")


def dot(a, b, dims):
    return lax.dot_general(a, b, dims, preferred_element_type=jnp.float32)


def room(extra):
    return pltpu.CompilerParams(vmem_limit_bytes=min((6 << 20) + extra, 60 << 20))


def own_kernel(groups, where_ref, k_ref, v_ref, mine_ref, *own_refs):
    heads = mine_ref.shape[0]
    for g in range(groups):
        for part, ref in enumerate((k_ref, v_ref)):
            to = slice((2 * g + part) * HEAD_SIZE, (2 * g + part + 1) * HEAD_SIZE)
            for h in range(heads):
                at = (h * groups + g) * HEAD_SIZE
                mine_ref[h, :, to] = ref[:, at : at + HEAD_SIZE]
            for o, own in enumerate(own_refs):
                at = pl.multiple_of(((where_ref[2] ^ o) * groups + g) * HEAD_SIZE, HEAD_SIZE)
                own[:, to] = ref[:, pl.ds(at, HEAD_SIZE)]


def far_kernel(groups, where_ref, mine_ref, kl_ref, vl_ref, far_ref):
    subs, heads = far_ref.shape[:2]
    for g in range(groups):
        for part, low in enumerate((kl_ref, vl_ref)):
            to = slice((2 * g + part) * HEAD_SIZE, (2 * g + part + 1) * HEAD_SIZE)
            for h in range(heads):
                at = (h * groups + g) * HEAD_SIZE
                mine = mine_ref[h, :, to]
                theirs = low[:, at : at + HEAD_SIZE]
                for dest in range(subs):
                    far_ref[dest, h, :, to] = jnp.where(where_ref[1] < dest, mine, theirs)


def attention_kernel(group, heads, where_ref, base_ref, start_ref, q_ref, do_ref, far_ref, *refs):
    own_refs, refs = refs[:heads], refs[heads:]
    o_ref, lse_ref, dq_ref, dfar_ref = refs[:4]
    down_refs, refs = refs[4 : 4 + heads], refs[4 + heads :]
    qs, dos, kw, vw, kt, vt, bias, p_all, ds_all = refs
    tok = q_ref.shape[0]
    scale = HEAD_SIZE ** (-0.5)
    subs = far_ref.shape[0]
    piece = tok // heads
    for h in range(group):
        cols = slice(h * HEAD_SIZE, (h + 1) * HEAD_SIZE)
        qs[h * tok : (h + 1) * tok, :] = q_ref[:, cols]
        dos[h * tok : (h + 1) * tok, :] = do_ref[:, cols]
    for b in range(subs):
        rows = slice(b * tok, (b + 1) * tok)
        kw[rows, :] = far_ref[b, :, :HEAD_SIZE]
        vw[rows, :] = far_ref[b, :, HEAD_SIZE:]

    def held(o):
        return pl.ds(pl.multiple_of(subs * tok + (where_ref[2] ^ o) * piece, piece), piece)

    for o, ref in enumerate(own_refs):
        kw[held(o), :] = ref[:, :HEAD_SIZE]
        vw[held(o), :] = ref[:, HEAD_SIZE:]
    kt[...] = kw[...].T
    vt[...] = vw[...].T

    @pl.when(pl.program_id(0) == 0)
    def _():
        row = lax.broadcasted_iota(jnp.int32, (tok, tok), 0)
        query = base_ref[subs] + lax.broadcasted_iota(jnp.int32, (tok, tok), 1)
        for b in range(subs + 1):
            place = base_ref[b] + row
            allowed = (place >= start_ref[...]) & (place <= query)
            bias[b * tok : (b + 1) * tok, :] = jnp.where(allowed, 0.0, MASK)

    pair = 2
    width = pair * tok
    count = group // pair

    def at(i):
        return slice(i * width, (i + 1) * width)

    def scores(i):
        return dot(kw[...], qs[at(i), :], NT)

    def finish(i, p, inv, dp):
        low = p_all[:, at(i)]
        ot = dot(vt[...], low, NN)
        outs = [ot[:, j * tok : (j + 1) * tok].T.astype(jnp.bfloat16) for j in range(pair)]
        turned = ot.astype(jnp.bfloat16).astype(jnp.float32)
        grad = dos[at(i), :].T.astype(jnp.float32)
        delta = jnp.sum(turned * grad, axis=0, keepdims=True)
        ds_all[:, at(i)] = ((p * inv) * (dp - delta)).astype(jnp.bfloat16)
        dqt = dot(kt[...], ds_all[:, at(i)], NN) * scale
        for j in range(pair):
            h = i * pair + j
            cols = slice(h * HEAD_SIZE, (h + 1) * HEAD_SIZE)
            o_ref[:, cols] = outs[j]
            dq_ref[:, cols] = dqt[:, j * tok : (j + 1) * tok].T.astype(jnp.bfloat16)

    following = scores(0)
    waiting = []
    for i in range(count):
        s = following
        if i + 1 < count:
            following = scores(i + 1)
        dp = dot(vw[...], dos[at(i), :], NT)
        s = s * (scale * LOG2E) + jnp.concatenate([bias[...]] * pair, axis=1)
        top = jnp.max(s, axis=0, keepdims=True)
        p = jnp.exp2(s - top)
        total = jnp.sum(p, axis=0, keepdims=True)
        inv = 1.0 / total
        lse = (top + jnp.log2(total)) * LN2
        for j in range(pair):
            lse_ref[i * pair + j : i * pair + j + 1, :] = lse[:, j * tok : (j + 1) * tok]
        p_all[:, at(i)] = (p * inv).astype(jnp.bfloat16)

        waiting.append((i, p, inv, dp))
        if i + 1 == count:
            dv = dot(p_all[...], dos[...], NN).astype(jnp.bfloat16)
        if len(waiting) > 0:
            finish(*waiting.pop(0))
    while waiting:
        finish(*waiting.pop(0))
    kw[...] = (dot(ds_all[...], qs[...], NN) * scale).astype(jnp.bfloat16)
    vw[...] = dv
    for b in range(subs):
        rows = slice(b * tok, (b + 1) * tok)
        dfar_ref[b, :, :HEAD_SIZE] = kw[rows, :]
        dfar_ref[b, :, HEAD_SIZE:] = vw[rows, :]
    for o, ref in enumerate(down_refs):
        ref[:, :HEAD_SIZE] = kw[held(o), :]
        ref[:, HEAD_SIZE:] = vw[held(o), :]


def attend(groups, where, base, start, queries, grads, far, own):
    tok = queries.shape[0]
    group = queries.shape[1] // HEAD_SIZE // groups
    keys = (1 + far.shape[0]) * tok
    column = pl.BlockSpec((tok, group * HEAD_SIZE), lambda g: (0, g))
    many = pl.BlockSpec((far.shape[0], tok, 2 * HEAD_SIZE), lambda g: (0, 0, g))
    single = pl.BlockSpec((own[0].shape[0], 2 * HEAD_SIZE), lambda g: (0, g))
    scalar = pl.BlockSpec(memory_space=pltpu.SMEM)
    wide = jax.ShapeDtypeStruct(queries.shape, jnp.bfloat16)
    rows = group * tok
    bf = lambda *shape: pltpu.VMEM(shape, jnp.bfloat16)
    return pl.pallas_call(
        functools.partial(attention_kernel, group, len(own)),
        grid=(groups,),
        out_shape=[
            wide,
            jax.ShapeDtypeStruct((groups * group, tok), jnp.float32),
            wide,
            jax.ShapeDtypeStruct(far.shape, jnp.bfloat16),
        ]
        + [jax.ShapeDtypeStruct(x.shape, jnp.bfloat16) for x in own],
        in_specs=[
            scalar,
            scalar,
            pl.BlockSpec((1, tok), lambda g: (0, 0)),
            column,
            column,
            many,
        ]
        + [single] * len(own),
        out_specs=[column, pl.BlockSpec((group, tok), lambda g: (g, 0)), column, many]
        + [single] * len(own),
        scratch_shapes=[
            bf(rows, HEAD_SIZE),
            bf(rows, HEAD_SIZE),
            bf(keys, HEAD_SIZE),
            bf(keys, HEAD_SIZE),
            bf(HEAD_SIZE, keys),
            bf(HEAD_SIZE, keys),
            pltpu.VMEM((keys, tok), jnp.float32),
            bf(keys, rows),
            bf(keys, rows),
        ],
        cost_estimate=pl.CostEstimate(
            flops=12 * groups * rows * keys * HEAD_SIZE,
            bytes_accessed=16 * groups * rows * HEAD_SIZE,
            transcendentals=groups * rows * keys,
        ),
        compiler_params=room(16 * keys * rows),
        name="attend",
    )(where, base, start, queries, grads, far, *own)


def collect_kernel(groups, where_ref, far_ref, *refs):
    heads = far_ref.shape[1]
    own_refs, (low_ref, sum_ref) = refs[:heads], refs[heads:]
    sub, head = where_ref[1], where_ref[2]
    pieces = [(g, part) for g in range(groups) for part in range(2)]
    for o, ref in enumerate(own_refs):
        for g, part in pieces:
            at = pl.multiple_of(((head ^ o) * groups + g) * HEAD_SIZE, HEAD_SIZE)
            to = (2 * g + part) * HEAD_SIZE
            sum_ref[part, :, pl.ds(at, HEAD_SIZE)] = ref[
                :, to : to + HEAD_SIZE
            ].astype(jnp.float32)
    for h in range(heads):
        for g, part in pieces:
            at = (h * groups + g) * HEAD_SIZE
            cols = slice(at, at + HEAD_SIZE)
            to = (2 * g + part) * HEAD_SIZE
            own = sum_ref[part, :, cols]
            low = jnp.zeros_like(own)
            for s in range(far_ref.shape[0]):
                got = far_ref[s, h, :, to : to + HEAD_SIZE].astype(jnp.float32)
                own = own + jnp.where(sub < s, got, 0.0)
                low = low + jnp.where(sub < s, 0.0, got)
            sum_ref[part, :, cols] = own
            low_ref[part, :, cols] = low.astype(jnp.bfloat16)


def finish_kernel(low_ref, sum_ref, dk_ref, dv_ref):
    for part, ref in enumerate((dk_ref, dv_ref)):
        ref[...] = (sum_ref[part] + low_ref[part].astype(jnp.float32)).astype(jnp.bfloat16)


def body(queries, key_rows, value_rows, grad_out, doc_ids, block_owner):
    subs = lax.axis_size("sub")
    shards = 2 * subs
    heads = lax.axis_size("head")
    half, sub, head = (lax.axis_index(name) for name in (*CTX, "head"))
    shard = half * subs + sub
    tok = queries.shape[0]
    rows = key_rows.shape[0]
    block = tok // shards
    groups = key_rows.shape[1] // HEAD_SIZE // heads
    width = 2 * groups * HEAD_SIZE
    where = jnp.stack([half, sub, head])
    vmem = pl.BlockSpec(memory_space=pltpu.VMEM)
    scalar = pl.BlockSpec(memory_space=pltpu.SMEM)

    def swap(x, axis, d):
        return lax.ppermute(x, axis, [(i, i ^ d) for i in range(lax.axis_size(axis))])

    low_keys, low_values = swap(key_rows, "half", 1), swap(value_rows, "half", 1)
    mine, *own = pl.pallas_call(
        functools.partial(own_kernel, groups),
        out_shape=[jax.ShapeDtypeStruct((heads, rows, width), jnp.bfloat16)]
        + [jax.ShapeDtypeStruct((rows, width), jnp.bfloat16)] * heads,
        in_specs=[scalar] + [vmem] * 2,
        cost_estimate=pl.CostEstimate(
            flops=1 << 21, bytes_accessed=12 * key_rows.size, transcendentals=0
        ),
        compiler_params=room(16 * key_rows.size),
        name="own",
    )(where, key_rows, value_rows)
    own = [own[0]] + [swap(own[o], "head", o) for o in range(1, heads)]
    packed = pl.pallas_call(
        functools.partial(far_kernel, groups),
        out_shape=jax.ShapeDtypeStruct((subs, heads, rows, width), jnp.bfloat16),
        in_specs=[scalar] + [vmem] * 3,
        compiler_params=room(8 * subs * rows * heads * width),
        name="far",
    )(where, mine, low_keys, low_values)
    far = lax.all_to_all(
        packed.reshape(subs * heads, rows, width), ("sub", "head"), 0, 0, tiled=True
    ).reshape(subs, tok, width)
    mine = lax.dynamic_slice_in_dim(doc_ids, shard * tok, tok)
    start = jnp.sum((doc_ids[:, None] < mine[None, :]).astype(jnp.int32), axis=0, keepdims=True)
    each = jnp.arange(subs + 1, dtype=jnp.int32)
    base = half * subs + jnp.where(each < subs, each - jnp.where(each >= sub, subs, 0), sub)
    attention, norm, dq, dfar, *down = attend(
        groups, where, base * tok, start, queries, grad_out, far, own
    )
    parts = lax.all_to_all(
        dfar.reshape(subs * heads, rows, width), ("sub", "head"), 0, 0, tiled=True
    )
    down = [down[0]] + [swap(down[o], "head", o) for o in range(1, heads)]
    natural = norm.reshape(norm.shape[0], shards, block)
    owner = lax.dynamic_index_in_dim(block_owner, shard, 0, keepdims=False)
    order = jnp.stack([(sub ^ d) + subs * e for e in (half, 1 - half) for d in range(subs)])
    pick = owner[None, :] == order[:, None]
    routed = jnp.sum(jnp.where(pick[:, None, :, None], natural[None], 0.0), axis=2)
    routed = routed.reshape(2, subs, -1)
    across = swap(routed[1], "half", 1)
    ready = jnp.stack([routed[0], across], axis=1)
    near_lse = [ready[0]] + [swap(ready[d], "sub", d) for d in range(1, subs)]
    both = jnp.concatenate(near_lse, axis=0)
    source = jnp.stack([(sub ^ d) + subs * e for d in range(subs) for e in (half, 1 - half)])
    place = source[None, :] == jnp.arange(shards, dtype=jnp.int32)[:, None]
    owned = jnp.sum(jnp.where(place[:, :, None], both[None], 0.0), axis=1)
    owned = owned.reshape(shards, -1, block).transpose(1, 0, 2).reshape(-1, tok)
    low, sums = pl.pallas_call(
        functools.partial(collect_kernel, groups),
        out_shape=[
            jax.ShapeDtypeStruct((2, *key_rows.shape), jnp.bfloat16),
            jax.ShapeDtypeStruct((2, *key_rows.shape), jnp.float32),
        ],
        in_specs=[scalar] + [vmem] * (1 + heads),
        compiler_params=room(8 * far.size),
        name="collect",
    )(where, parts.reshape(subs, heads, rows, width), *down)
    low = swap(low, "half", 1)
    dk, dv = pl.pallas_call(
        finish_kernel,
        out_shape=[jax.ShapeDtypeStruct(key_rows.shape, jnp.bfloat16)] * 2,
        compiler_params=room(32 * key_rows.size),
        name="finish",
    )(low, sums)
    return (attention, owned, dq, dk, dv)


def solution(mesh):
    shards, heads = mesh.shape["ctx"], mesh.shape["head"]
    inner = Mesh(mesh.devices.reshape(2, shards // 2, heads), (*CTX, "head"))
    rows = P((*CTX, "head"), None)

    return jax.shard_map(
        body,
        mesh=inner,
        in_specs=(P(CTX, "head"), rows, rows, P(CTX, "head"), P(), P()),
        out_specs=(P(CTX, "head"), P("head", CTX), P(CTX, "head"), rows, rows),
        check_vma=False,
    )
```

profile of v0, /device:TPU:0, one launch (start us, length us, event | category | flops | bytes accessed | tf_op | source)
XLA Modules:
  0.0 61.7 jit_solution(2978820133150976764)
XLA Ops:
  0.6 0.0 copy-start
  0.6 4.1 %collective-permute-start = (bf16[32,1024]{1,0:T(8,128)(2,1)}, bf16[32,1024]{1,0:T(8,128)(2,1)S(1)}, u32[]{:S(2)}, u32[]{:S(2)}) collective-permute-start(bf16[32,1024]{1,0:T(8,128)(2,1)} %k_ref.1), channel_id=1, source_target_pairs={{0,16},{16,0},{1,17},{17,1},{2,18},{18,2},{3,19},{19,3},{4,20},{20... | collective-permute-start | bytes 196616 | tf_op jit(solution)/shard_map/ppermute | solution.py:251
  4.8 0.1 collective-permute-start.1
  4.9 0.1 pad_add_fusion.where_ref
  4.9 0.0 copy-start.1
  4.9 0.8 %copy-done.1 = bf16[32,1024]{1,0:T(8,128)(2,1)S(1)} copy-done((bf16[32,1024]{1,0:T(8,128)(2,1)S(1)}, bf16[32,1024]{1,0:T(8,128)(2,1)}, u32[]{:S(2)}) %copy-start.1) | copy-done | bytes 65560
  5.8 0.0 copy-start.2
  5.8 0.8 %copy-done.2 = bf16[32,1024]{1,0:T(8,128)(2,1)S(1)} copy-done((bf16[32,1024]{1,0:T(8,128)(2,1)S(1)}, bf16[32,1024]{1,0:T(8,128)(2,1)}, u32[]{:S(2)}) %copy-start.2) | copy-done | bytes 65560
  6.6 0.6 own.1
  7.2 1.5 %collective-permute-done.kl_ref = bf16[32,1024]{1,0:T(8,128)(2,1)S(1)} collective-permute-done((bf16[32,1024]{1,0:T(8,128)(2,1)}, bf16[32,1024]{1,0:T(8,128)(2,1)S(1)}, u32[]{:S(2)}, u32[]{:S(2)}) %collective-permute-start) | collective-permute-done | bytes 65568 | tf_op jit(solution)/shard_map/ppermute | solution.py:251
  8.7 2.7 %collective-permute-done.1.vl_ref = bf16[32,1024]{1,0:T(8,128)(2,1)S(1)} collective-permute-done((bf16[32,1024]{1,0:T(8,128)(2,1)}, bf16[32,1024]{1,0:T(8,128)(2,1)S(1)}, u32[]{:S(2)}, u32[]{:S(2)}) %collective-permute-start.1) | collective-permute-done | bytes 65568 | tf_op jit(solution)/shard_map/ppermute | solution.py:251
  11.4 1.4 %far.1 = bf16[4,4,32,512]{3,2,1,0:T(8,128)(2,1)} custom-call(s32[3]{0:T(128)S(1)} %pad_add_fusion.where_ref, bf16[4,32,512]{2,1,0:T(8,128)(2,1)S(1)} %get-tuple-element.22.mine_ref, bf16[32,1024]{1,0:T(8,128)(2,1)S(1)} %collective-permute-done.kl_ref, bf16[32,1024]{1,0:T(8,128)(2,1)S(1)} %collective-permute-done.1.vl_ref), custom_call_target="tpu_custom_call" | custom-call | tf_op jit(solution)/shard_map/far/pallas_call | solution.py:266
  12.9 0.0 copy-start.3
  12.9 0.0 copy-start.4
  12.9 4.2 %all-to-all-start = ((bf16[16,32,512]{2,1,0:T(8,128)(2,1)}), bf16[16,32,512]{2,1,0:T(8,128)(2,1)S(1)}, u32[]{:S(2)}, u32[]{:S(2)}) async-start(bf16[16,32,512]{2,1,0:T(8,128)(2,1)} %bitcast.4), calls=%async_computation | async-start | bytes 1048576 | tf_op jit(solution)/shard_map/all_to_all | solution.py:273
  17.0 0.4 collective-permute-start.2
  17.4 1.6 %collective-permute-start.3 = (bf16[32,512]{1,0:T(8,128)(2,1)S(1)}, bf16[32,512]{1,0:T(8,128)(2,1)S(1)}, u32[]{:S(2)}, u32[]{:S(2)}) collective-permute-start(bf16[32,512]{1,0:T(8,128)(2,1)S(1)} %get-tuple-element.25), channel_id=1, source_target_pairs={{0,2},{1,3},{2,0},{3,1},{4,6},{5,7},{6,4},{7,5},{8,10},{9,11},{10,... | collective-permute-start | bytes 98312 | tf_op jit(solution)/shard_map/ppermute | solution.py:251
  19.1 0.0 collective-permute-start.4
  19.1 0.0 copy-start.5
  19.1 0.7 %copy-done.5 = s32[1024]{0:T(1024)S(1)} copy-done((s32[1024]{0:T(1024)S(1)}, s32[1024]{0:T(1024)}, u32[]{:S(2)}) %copy-start.5) | copy-done | bytes 4120
  19.8 0.1 dynamic_slice.7
  19.8 0.2 convert_reduce_fusion
  20.1 0.1 stack.69
  20.2 0.0 collective-permute-done.2.refs_1_
  20.2 6.6 %collective-permute-done.3.refs_2_ = bf16[32,512]{1,0:T(8,128)(2,1)S(1)} collective-permute-done((bf16[32,512]{1,0:T(8,128)(2,1)S(1)}, bf16[32,512]{1,0:T(8,128)(2,1)S(1)}, u32[]{:S(2)}, u32[]{:S(2)}) %collective-permute-start.3) | collective-permute-done | bytes 32800 | tf_op jit(solution)/shard_map/ppermute | solution.py:251
  26.8 0.0 collective-permute-done.4.refs_3_
  26.8 0.7 %all-to-all-done = bf16[16,32,512]{2,1,0:T(8,128)(2,1)S(1)} async-done(((bf16[16,32,512]{2,1,0:T(8,128)(2,1)}), bf16[16,32,512]{2,1,0:T(8,128)(2,1)S(1)}, u32[]{:S(2)}, u32[]{:S(2)}) %all-to-all-start) | async-done | bytes 524320 | tf_op jit(solution)/shard_map/all_to_all | solution.py:273
  27.6 0.0 copy-done.3
  27.6 0.0 copy-done.4
  27.6 7.7 %attend.1 = (bf16[128,2048]{1,0:T(8,128)(2,1)}, f32[16,128]{1,0:T(8,128)S(1)}, bf16[128,2048]{1,0:T(8,128)(2,1)}, bf16[4,128,512]{2,1,0:T(8,128)(2,1)}, bf16[32,...) custom-call(s32[3]{0:T(128)S(1)} %pad_add_fusion.where_ref, ...), custom_call_target="tpu_custom_call" | custom-call | flops 2013265920 | bytes 4194304 | tf_op jit(solution)/shard_map/attend/pallas_call | solution.py:161
  35.2 3.6 %all-to-all-start.1 = ((bf16[16,32,512]{2,1,0:T(8,128)(2,1)}), bf16[16,32,512]{2,1,0:T(8,128)(2,1)S(1)}, u32[]{:S(2)}, u32[]{:S(2)}) async-start(bf16[16,32,512]{2,1,0:T(8,128)(2,1)} %bitcast.20), calls=%async_computation.1 | async-start | bytes 1048576 | tf_op jit(solution)/shard_map/all_to_all | solution.py:283
  38.8 0.0 copy-done
  38.8 0.1 broadcast_compare_fusion
  38.9 0.1 broadcast_in_dim.66
  39.0 0.2 select_reduce_fusion
  39.2 0.1 squeeze.17
  39.3 3.2 %collective-permute-start.5 = (f32[4,256]{1,0:T(4,128)S(1)}, f32[4,256]{1,0:T(4,128)S(1)}, u32[]{:S(2)}, u32[]{:S(2)}) collective-permute-start(f32[4,256]{1,0:T(4,128)S(1)} %squeeze.17), channel_id=1, source_target_pairs={{0,16},{16,0},{1,17},{17,1},{2,18},{18,2},{3,19},{19,3},{4,20},{20... | collective-permute-start | bytes 12296 | tf_op jit(solution)/shard_map/ppermute | solution.py:251
  42.5 0.1 stack.68
  42.6 0.0 collective-permute-start.9
  42.6 1.9 %collective-permute-start.10 = (bf16[32,512]{1,0:T(8,128)(2,1)S(1)}, bf16[32,512]{1,0:T(8,128)(2,1)S(1)}, u32[]{:S(2)}, u32[]{:S(2)}) collective-permute-start(bf16[32,512]{1,0:T(8,128)(2,1)S(1)} %get-tuple-element.33), channel_id=1, source_target_pairs={{0,2},{1,3},{2,0},{3,1},{4,6},{5,7},{6,4},{7,5},{8,10},{9,11},{10,... | collective-permute-start | bytes 98312 | tf_op jit(solution)/shard_map/ppermute | solution.py:251
  44.5 0.0 collective-permute-start.11
  44.5 0.1 stack_squeeze.3
  44.6 0.8 %collective-permute-done.5 = f32[4,256]{1,0:T(4,128)S(1)} collective-permute-done((f32[4,256]{1,0:T(4,128)S(1)}, f32[4,256]{1,0:T(4,128)S(1)}, u32[]{:S(2)}, u32[]{:S(2)}) %collective-permute-start.5) | collective-permute-done | bytes 4128 | tf_op jit(solution)/shard_map/ppermute | solution.py:251
  45.5 5.3 %collective-permute-start.7 = (f32[2,256]{1,0:T(2,128)S(1)}, f32[2,256]{1,0:T(2,128)S(1)}, u32[]{:S(2)}, u32[]{:S(2)}) collective-permute-start(f32[2,256]{1,0:T(2,128)S(1)} %bitcast.40), channel_id=1, source_target_pairs={{0,8},{4,12},{8,0},{12,4},{1,9},{5,13},{9,1},{13,5},{2,10},{6,14},... | collective-permute-start | bytes 6152 | tf_op jit(solution)/shard_map/ppermute | solution.py:251
  50.8 1.0 %collective-permute-start.8 = (f32[2,256]{1,0:T(2,128)S(1)}, f32[2,256]{1,0:T(2,128)S(1)}, u32[]{:S(2)}, u32[]{:S(2)}) collective-permute-start(f32[2,256]{1,0:T(2,128)S(1)} %bitcast.39), channel_id=1, source_target_pairs={{0,12},{4,8},{8,4},{12,0},{1,13},{5,9},{9,5},{13,1},{2,14},{6,10},... | collective-permute-start | bytes 6152 | tf_op jit(solution)/shard_map/ppermute | solution.py:251
  51.8 0.0 collective-permute-done.9.refs_1_
  51.8 0.5 collective-permute-start.6
  52.4 0.0 collective-permute-done.10.refs_2_
  52.4 0.0 collective-permute-done.11.refs_3_
  52.4 0.0 all-to-all-done.1
  52.4 0.7 %collect.1 = (bf16[2,32,1024]{2,1,0:T(8,128)(2,1)S(1)}, f32[2,32,1024]{2,1,0:T(8,128)S(1)}) custom-call(s32[3]{0:T(128)S(1)} %pad_add_fusion.where_ref, bf16[4,4,32,512]{3,2,1,0:T(8,128)(2,1)S(1)} %bitcast.32, bf16[32,512]{1,0:T(8,128)(2,1)S(1)} %get-tuple-element.31.refs_0_, bf16[32,512]{1,0:T(8,128)(2,1)S(1)} %collective-permute-done.9.refs_1_, ...), custom_call_target="tpu_custom_call" | custom-call | tf_op jit(solution)/shard_map/collect/pallas_call | solution.py:301
  53.2 0.2 collective-permute-start.12
  53.3 0.0 collective-permute-done.7
  53.3 2.0 %collective-permute-done.8 = f32[2,256]{1,0:T(2,128)S(1)} collective-permute-done((f32[2,256]{1,0:T(2,128)S(1)}, f32[2,256]{1,0:T(2,128)S(1)}, u32[]{:S(2)}, u32[]{:S(2)}) %collective-permute-start.8) | collective-permute-done | bytes 2080 | tf_op jit(solution)/shard_map/ppermute | solution.py:251
  55.3 0.1 collective-permute-done.6
  55.4 0.1 select_reduce_fusion.1
  55.5 0.1 reshape.84
  55.6 0.7 %reshape.85 = f32[16,128]{1,0:T(8,128)} reshape(f32[16,8,16]{2,1,0:T(8,128)S(1)} %copy.15) | data formatting | bytes 16384 | tf_op jit(solution)/shard_map/reshape | solution.py:300
  56.3 4.7 %collective-permute-done.12.low_ref = bf16[2,32,1024]{2,1,0:T(8,128)(2,1)S(1)} collective-permute-done((bf16[2,32,1024]{2,1,0:T(8,128)(2,1)S(1)}, bf16[2,32,1024]{2,1,0:T(8,128)(2,1)S(1)}, u32[]{:S(2)}, u32[]{:S(2)}) %collective-permute-start.12) | collective-permute-done | bytes 131104 | tf_op jit(solution)/shard_map/ppermute | solution.py:251
  61.0 0.7 %finish.1 = (bf16[32,1024]{1,0:T(8,128)(2,1)}, bf16[32,1024]{1,0:T(8,128)(2,1)}) custom-call(bf16[2,32,1024]{2,1,0:T(8,128)(2,1)S(1)} %collective-permute-done.12.low_ref, f32[2,32,1024]{2,1,0:T(8,128)S(1)} %get-tuple-element.36.sum_ref), custom_call_target="tpu_custom_call" | custom-call | tf_op jit(solution)/shard_map/finish/pallas_call | solution.py:312
  (11 shorter events, 0.1 us)
Async XLA Ops:
  0.6 38.2 %copy-start = (s32[8,8]{1,0:T(8,128)S(1)}, s32[8,8]{1,0:T(8,128)}, u32[]{:S(2)}) copy-start(s32[8,8]{1,0:T(8,128)} %param.11) | copy-start | bytes 772
  0.6 8.1 %collective-permute-start = (bf16[32,1024]{1,0:T(8,128)(2,1)}, bf16[32,1024]{1,0:T(8,128)(2,1)S(1)}, u32[]{:S(2)}, u32[]{:S(2)}) collective-permute-start(bf16[32,1024]{1,0:T(8,128)(2,1)} %k_ref.1), channel_id=1, source_target_pairs={{0,16},{16,0},{1,17},{17,1},{2,18},{18,2},{3,19},{19,3},{4,20},{20... | collective-permute-start | bytes 196616 | tf_op jit(solution)/shard_map/ppermute | solution.py:251
  4.8 6.7 %collective-permute-start.1 = (bf16[32,1024]{1,0:T(8,128)(2,1)}, bf16[32,1024]{1,0:T(8,128)(2,1)S(1)}, u32[]{:S(2)}, u32[]{:S(2)}) collective-permute-start(bf16[32,1024]{1,0:T(8,128)(2,1)} %v_ref.1), channel_id=1, source_target_pairs={{0,16},{16,0},{1,17},{17,1},{2,18},{18,2},{3,19},{19,3},{4,20},{20... | collective-permute-start | bytes 196616 | tf_op jit(solution)/shard_map/ppermute | solution.py:251
  4.9 0.8 %copy-start.1 = (bf16[32,1024]{1,0:T(8,128)(2,1)S(1)}, bf16[32,1024]{1,0:T(8,128)(2,1)}, u32[]{:S(2)}) copy-start(bf16[32,1024]{1,0:T(8,128)(2,1)} %k_ref.1) | copy-start | bytes 196612
  5.8 0.8 %copy-start.2 = (bf16[32,1024]{1,0:T(8,128)(2,1)S(1)}, bf16[32,1024]{1,0:T(8,128)(2,1)}, u32[]{:S(2)}) copy-start(bf16[32,1024]{1,0:T(8,128)(2,1)} %v_ref.1) | copy-start | bytes 196612
  12.9 14.7 %copy-start.3 = (bf16[128,2048]{1,0:T(8,128)(2,1)S(1)}, bf16[128,2048]{1,0:T(8,128)(2,1)}, u32[]{:S(2)}) copy-start(bf16[128,2048]{1,0:T(8,128)(2,1)} %q_ref.1) | copy-start | bytes 1572868
  12.9 14.7 %copy-start.4 = (bf16[128,2048]{1,0:T(8,128)(2,1)S(1)}, bf16[128,2048]{1,0:T(8,128)(2,1)}, u32[]{:S(2)}) copy-start(bf16[128,2048]{1,0:T(8,128)(2,1)} %do_ref.1) | copy-start | bytes 1572868
  12.9 14.7 %all-to-all-start = ((bf16[16,32,512]{2,1,0:T(8,128)(2,1)}), bf16[16,32,512]{2,1,0:T(8,128)(2,1)S(1)}, u32[]{:S(2)}, u32[]{:S(2)}) async-start(bf16[16,32,512]{2,1,0:T(8,128)(2,1)} %bitcast.4), calls=%async_computation | async-start | bytes 1048576 | tf_op jit(solution)/shard_map/all_to_all | solution.py:273
  17.0 3.1 %collective-permute-start.2 = (bf16[32,512]{1,0:T(8,128)(2,1)S(1)}, bf16[32,512]{1,0:T(8,128)(2,1)S(1)}, u32[]{:S(2)}, u32[]{:S(2)}) collective-permute-start(bf16[32,512]{1,0:T(8,128)(2,1)S(1)} %get-tuple-element.24), channel_id=1, source_target_pairs={{0,1},{1,0},{2,3},{3,2},{4,5},{5,4},{6,7},{7,6},{8,9},{9,8},{10,11... | collective-permute-start | bytes 98312 | tf_op jit(solution)/shard_map/ppermute | solution.py:251
  17.4 9.4 %collective-permute-start.3 = (bf16[32,512]{1,0:T(8,128)(2,1)S(1)}, bf16[32,512]{1,0:T(8,128)(2,1)S(1)}, u32[]{:S(2)}, u32[]{:S(2)}) collective-permute-start(bf16[32,512]{1,0:T(8,128)(2,1)S(1)} %get-tuple-element.25), channel_id=1, source_target_pairs={{0,2},{1,3},{2,0},{3,1},{4,6},{5,7},{6,4},{7,5},{8,10},{9,11},{10,... | collective-permute-start | bytes 98312 | tf_op jit(solution)/shard_map/ppermute | solution.py:251
  19.1 7.7 %collective-permute-start.4 = (bf16[32,512]{1,0:T(8,128)(2,1)S(1)}, bf16[32,512]{1,0:T(8,128)(2,1)S(1)}, u32[]{:S(2)}, u32[]{:S(2)}) collective-permute-start(bf16[32,512]{1,0:T(8,128)(2,1)S(1)} %get-tuple-element.26), channel_id=1, source_target_pairs={{0,3},{1,2},{2,1},{3,0},{4,7},{5,6},{6,5},{7,4},{8,11},{9,10},{10,... | collective-permute-start | bytes 98312 | tf_op jit(solution)/shard_map/ppermute | solution.py:251
  19.1 0.7 %copy-start.5 = (s32[1024]{0:T(1024)S(1)}, s32[1024]{0:T(1024)}, u32[]{:S(2)}) copy-start(s32[1024]{0:T(1024)} %param.10) | copy-start | bytes 12292
  35.2 17.2 %all-to-all-start.1 = ((bf16[16,32,512]{2,1,0:T(8,128)(2,1)}), bf16[16,32,512]{2,1,0:T(8,128)(2,1)S(1)}, u32[]{:S(2)}, u32[]{:S(2)}) async-start(bf16[16,32,512]{2,1,0:T(8,128)(2,1)} %bitcast.20), calls=%async_computation.1 | async-start | bytes 1048576 | tf_op jit(solution)/shard_map/all_to_all | solution.py:283
  39.3 6.1 %collective-permute-start.5 = (f32[4,256]{1,0:T(4,128)S(1)}, f32[4,256]{1,0:T(4,128)S(1)}, u32[]{:S(2)}, u32[]{:S(2)}) collective-permute-start(f32[4,256]{1,0:T(4,128)S(1)} %squeeze.17), channel_id=1, source_target_pairs={{0,16},{16,0},{1,17},{17,1},{2,18},{18,2},{3,19},{19,3},{4,20},{20... | collective-permute-start | bytes 12296 | tf_op jit(solution)/shard_map/ppermute | solution.py:251
  42.6 9.2 %collective-permute-start.9 = (bf16[32,512]{1,0:T(8,128)(2,1)S(1)}, bf16[32,512]{1,0:T(8,128)(2,1)S(1)}, u32[]{:S(2)}, u32[]{:S(2)}) collective-permute-start(bf16[32,512]{1,0:T(8,128)(2,1)S(1)} %get-tuple-element.32), channel_id=1, source_target_pairs={{0,1},{1,0},{2,3},{3,2},{4,5},{5,4},{6,7},{7,6},{8,9},{9,8},{10,11... | collective-permute-start | bytes 98312 | tf_op jit(solution)/shard_map/ppermute | solution.py:251
  42.6 9.8 %collective-permute-start.10 = (bf16[32,512]{1,0:T(8,128)(2,1)S(1)}, bf16[32,512]{1,0:T(8,128)(2,1)S(1)}, u32[]{:S(2)}, u32[]{:S(2)}) collective-permute-start(bf16[32,512]{1,0:T(8,128)(2,1)S(1)} %get-tuple-element.33), channel_id=1, source_target_pairs={{0,2},{1,3},{2,0},{3,1},{4,6},{5,7},{6,4},{7,5},{8,10},{9,11},{10,... | collective-permute-start | bytes 98312 | tf_op jit(solution)/shard_map/ppermute | solution.py:251
  44.5 7.9 %collective-permute-start.11 = (bf16[32,512]{1,0:T(8,128)(2,1)S(1)}, bf16[32,512]{1,0:T(8,128)(2,1)S(1)}, u32[]{:S(2)}, u32[]{:S(2)}) collective-permute-start(bf16[32,512]{1,0:T(8,128)(2,1)S(1)} %get-tuple-element.34), channel_id=1, source_target_pairs={{0,3},{1,2},{2,1},{3,0},{4,7},{5,6},{6,5},{7,4},{8,11},{9,10},{10,... | collective-permute-start | bytes 98312 | tf_op jit(solution)/shard_map/ppermute | solution.py:251
  45.5 7.8 %collective-permute-start.7 = (f32[2,256]{1,0:T(2,128)S(1)}, f32[2,256]{1,0:T(2,128)S(1)}, u32[]{:S(2)}, u32[]{:S(2)}) collective-permute-start(f32[2,256]{1,0:T(2,128)S(1)} %bitcast.40), channel_id=1, source_target_pairs={{0,8},{4,12},{8,0},{12,4},{1,9},{5,13},{9,1},{13,5},{2,10},{6,14},... | collective-permute-start | bytes 6152 | tf_op jit(solution)/shard_map/ppermute | solution.py:251
  50.8 4.5 %collective-permute-start.8 = (f32[2,256]{1,0:T(2,128)S(1)}, f32[2,256]{1,0:T(2,128)S(1)}, u32[]{:S(2)}, u32[]{:S(2)}) collective-permute-start(f32[2,256]{1,0:T(2,128)S(1)} %bitcast.39), channel_id=1, source_target_pairs={{0,12},{4,8},{8,4},{12,0},{1,13},{5,9},{9,5},{13,1},{2,14},{6,10},... | collective-permute-start | bytes 6152 | tf_op jit(solution)/shard_map/ppermute | solution.py:251
  51.8 3.6 %collective-permute-start.6 = (f32[2,256]{1,0:T(2,128)S(1)}, f32[2,256]{1,0:T(2,128)S(1)}, u32[]{:S(2)}, u32[]{:S(2)}) collective-permute-start(f32[2,256]{1,0:T(2,128)S(1)} %bitcast.38), channel_id=1, source_target_pairs={{0,4},{4,0},{8,12},{12,8},{1,5},{5,1},{9,13},{13,9},{2,6},{6,2},{1... | collective-permute-start | bytes 6152 | tf_op jit(solution)/shard_map/ppermute | solution.py:251
  53.2 7.9 %collective-permute-start.12 = (bf16[2,32,1024]{2,1,0:T(8,128)(2,1)S(1)}, bf16[2,32,1024]{2,1,0:T(8,128)(2,1)S(1)}, u32[]{:S(2)}, u32[]{:S(2)}) collective-permute-start(bf16[2,32,1024]{2,1,0:T(8,128)(2,1)S(1)} %get-tuple-element.35), channel_id=1, source_target_pairs={{0,16},{16,0},{1,17},{17,1},{2,18},{18,2},{3,19},{19,3},{4,20},{20... | collective-permute-start | bytes 393224 | tf_op jit(solution)/shard_map/ppermute | solution.py:251
where the time goes:
time: 62.1 us; the launch traced here: 61.7 us
  starting transfers between devices  26.2 us (42%)
  waiting for transfers between devices  19.2 us (31%)
  Pallas kernels  11.1 us (18%)
  local copies, waits for them, and re-layouts  3.68 us (6%)
  between operations  0.83 us (1%)
  other arithmetic  0.71 us (1%)
    ppermute x13, waiting for transfers between devices, swap(): lax.ppermute(x, axis, [(i, i ^ d) for i in range(lax.axis_size(axis))])  18.5 us
    ppermute x13, starting transfers between devices, swap(): lax.ppermute(x, axis, [(i, i ^ d) for i in range(lax.axis_size(axis))])  18.4 us
    pallas_call x1, Pallas kernels, attend(): pl.pallas_call(functools.partial(attention_kernel, group, len(own)), grid...  7.66 us
    all_to_all x1, starting transfers between devices, body(): lax.all_to_all(packed.reshape(subs * heads, rows, width), ('sub', 'head')...  4.16 us
    all_to_all x1, starting transfers between devices, body(): lax.all_to_all(dfar.reshape(subs * heads, rows, width), ('sub', 'head'),...  3.57 us
    unnamed x16, local copies, waits for them, and re-layouts  2.39 us
    pallas_call x1, Pallas kernels, body(): pl.pallas_call(functools.partial(far_kernel, groups), out_shape=jax.Shape...  1.41 us
  transfers between devices with their start and end apart: 15, of which 8 were waited for; matrix products, arithmetic and copies ran while one was open for 3% of the time, Pallas kernels for 2%

commit v1 on v0

--- a/solution.py
+++ b/solution.py
@@ -51,35 +51,48 @@
                     far_ref[dest, h, :, to] = jnp.where(where_ref[1] < dest, mine, theirs)
 
 
-def attention_kernel(group, heads, where_ref, base_ref, start_ref, q_ref, do_ref, far_ref, *refs):
+def attention_kernel(group, groups, heads, *refs):
+    scratch = refs[-8 * groups :]
+    bias, refs = refs[-8 * groups - 1], refs[: -8 * groups - 1]
+    for g in range(groups):
+        one_group(g, group, heads, bias, scratch[8 * g : 8 * g + 8], *refs)
+
+
+def one_group(
+    g, group, heads, bias, scratch, where_ref, base_ref, start_ref, q_ref, do_ref, far_ref, *refs
+):
     own_refs, refs = refs[:heads], refs[heads:]
     o_ref, lse_ref, dq_ref, dfar_ref = refs[:4]
-    down_refs, refs = refs[4 : 4 + heads], refs[4 + heads :]
-    qs, dos, kw, vw, kt, vt, bias, p_all, ds_all = refs
+    down_refs = refs[4:]
+    qs, dos, kw, vw, kt, vt, p_all, ds_all = scratch
+    key_cols = slice(2 * g * HEAD_SIZE, (2 * g + 1) * HEAD_SIZE)
+    value_cols = slice((2 * g + 1) * HEAD_SIZE, (2 * g + 2) * HEAD_SIZE)
+
+    def columns(h):
+        return slice((g * group + h) * HEAD_SIZE, (g * group + h + 1) * HEAD_SIZE)
+
     tok = q_ref.shape[0]
     scale = HEAD_SIZE ** (-0.5)
     subs = far_ref.shape[0]
     piece = tok // heads
     for h in range(group):
-        cols = slice(h * HEAD_SIZE, (h + 1) * HEAD_SIZE)
-        qs[h * tok : (h + 1) * tok, :] = q_ref[:, cols]
-        dos[h * tok : (h + 1) * tok, :] = do_ref[:, cols]
+        qs[h * tok : (h + 1) * tok, :] = q_ref[:, columns(h)]
+        dos[h * tok : (h + 1) * tok, :] = do_ref[:, columns(h)]
     for b in range(subs):
         rows = slice(b * tok, (b + 1) * tok)
-        kw[rows, :] = far_ref[b, :, :HEAD_SIZE]
-        vw[rows, :] = far_ref[b, :, HEAD_SIZE:]
+        kw[rows, :] = far_ref[b, :, key_cols]
+        vw[rows, :] = far_ref[b, :, value_cols]
 
     def held(o):
         return pl.ds(pl.multiple_of(subs * tok + (where_ref[2] ^ o) * piece, piece), piece)
 
     for o, ref in enumerate(own_refs):
-        kw[held(o), :] = ref[:, :HEAD_SIZE]
-        vw[held(o), :] = ref[:, HEAD_SIZE:]
+        kw[held(o), :] = ref[:, key_cols]
+        vw[held(o), :] = ref[:, value_cols]
     kt[...] = kw[...].T
     vt[...] = vw[...].T
 
-    @pl.when(pl.program_id(0) == 0)
-    def _():
+    if g == 0:
         row = lax.broadcasted_iota(jnp.int32, (tok, tok), 0)
         query = base_ref[subs] + lax.broadcasted_iota(jnp.int32, (tok, tok), 1)
         for b in range(subs + 1):
@@ -108,9 +121,8 @@
         dqt = dot(kt[...], ds_all[:, at(i)], NN) * scale
         for j in range(pair):
             h = i * pair + j
-            cols = slice(h * HEAD_SIZE, (h + 1) * HEAD_SIZE)
-            o_ref[:, cols] = outs[j]
-            dq_ref[:, cols] = dqt[:, j * tok : (j + 1) * tok].T.astype(jnp.bfloat16)
+            o_ref[:, columns(h)] = outs[j]
+            dq_ref[:, columns(h)] = dqt[:, j * tok : (j + 1) * tok].T.astype(jnp.bfloat16)
 
     following = scores(0)
     waiting = []
@@ -126,7 +138,8 @@
         inv = 1.0 / total
         lse = (top + jnp.log2(total)) * LN2
         for j in range(pair):
-            lse_ref[i * pair + j : i * pair + j + 1, :] = lse[:, j * tok : (j + 1) * tok]
+            h = g * group + i * pair + j
+            lse_ref[h : h + 1, :] = lse[:, j * tok : (j + 1) * tok]
         p_all[:, at(i)] = (p * inv).astype(jnp.bfloat16)
 
         waiting.append((i, p, inv, dp))
@@ -140,27 +153,24 @@
     vw[...] = dv
     for b in range(subs):
         rows = slice(b * tok, (b + 1) * tok)
-        dfar_ref[b, :, :HEAD_SIZE] = kw[rows, :]
-        dfar_ref[b, :, HEAD_SIZE:] = vw[rows, :]
+        dfar_ref[b, :, key_cols] = kw[rows, :]
+        dfar_ref[b, :, value_cols] = vw[rows, :]
     for o, ref in enumerate(down_refs):
-        ref[:, :HEAD_SIZE] = kw[held(o), :]
-        ref[:, HEAD_SIZE:] = vw[held(o), :]
+        ref[:, key_cols] = kw[held(o), :]
+        ref[:, value_cols] = vw[held(o), :]
 
 
 def attend(groups, where, base, start, queries, grads, far, own):
     tok = queries.shape[0]
     group = queries.shape[1] // HEAD_SIZE // groups
     keys = (1 + far.shape[0]) * tok
-    column = pl.BlockSpec((tok, group * HEAD_SIZE), lambda g: (0, g))
-    many = pl.BlockSpec((far.shape[0], tok, 2 * HEAD_SIZE), lambda g: (0, 0, g))
-    single = pl.BlockSpec((own[0].shape[0], 2 * HEAD_SIZE), lambda g: (0, g))
     scalar = pl.BlockSpec(memory_space=pltpu.SMEM)
+    vmem = pl.BlockSpec(memory_space=pltpu.VMEM)
     wide = jax.ShapeDtypeStruct(queries.shape, jnp.bfloat16)
     rows = group * tok
     bf = lambda *shape: pltpu.VMEM(shape, jnp.bfloat16)
     return pl.pallas_call(
-        functools.partial(attention_kernel, group, len(own)),
-        grid=(groups,),
+        functools.partial(attention_kernel, group, groups, len(own)),
         out_shape=[
             wide,
             jax.ShapeDtypeStruct((groups * group, tok), jnp.float32),
@@ -168,34 +178,25 @@
             jax.ShapeDtypeStruct(far.shape, jnp.bfloat16),
         ]
         + [jax.ShapeDtypeStruct(x.shape, jnp.bfloat16) for x in own],
-        in_specs=[
-            scalar,
-            scalar,
-            pl.BlockSpec((1, tok), lambda g: (0, 0)),
-            column,
-            column,
-            many,
-        ]
-        + [single] * len(own),
-        out_specs=[column, pl.BlockSpec((group, tok), lambda g: (g, 0)), column, many]
-        + [single] * len(own),
-        scratch_shapes=[
+        in_specs=[scalar] * 2 + [vmem] * (4 + len(own)),
+        scratch_shapes=[pltpu.VMEM((keys, tok), jnp.float32)]
+        + [
             bf(rows, HEAD_SIZE),
             bf(rows, HEAD_SIZE),
             bf(keys, HEAD_SIZE),
             bf(keys, HEAD_SIZE),
             bf(HEAD_SIZE, keys),
             bf(HEAD_SIZE, keys),
-            pltpu.VMEM((keys, tok), jnp.float32),
             bf(keys, rows),
             bf(keys, rows),
-        ],
+        ]
+        * groups,
         cost_estimate=pl.CostEstimate(
             flops=12 * groups * rows * keys * HEAD_SIZE,
             bytes_accessed=16 * groups * rows * HEAD_SIZE,
             transcendentals=groups * rows * keys,
         ),
-        compiler_params=room(16 * keys * rows),
+        compiler_params=room(16 * groups * keys * rows),
         name="attend",
     )(where, base, start, queries, grads, far, *own)
 
@@ -227,7 +228,23 @@
             low_ref[part, :, cols] = low.astype(jnp.bfloat16)
 
 
-def finish_kernel(low_ref, sum_ref, dk_ref, dv_ref):
+def route_kernel(block, spots_ref, *refs):
+    log_refs, outs = refs[:-2], refs[-2:]
+    rows, lanes = outs[0].shape
+    lane = lax.broadcasted_iota(jnp.int32, (rows, lanes), 1)
+    count = len(log_refs)
+    for k, out in enumerate(outs):
+        owned = jnp.zeros((rows, lanes), jnp.float32)
+        for d, ref in enumerate(log_refs):
+            to = spots_ref[d] * block
+            at = spots_ref[count * (1 + k) + d] * block
+            turned = pltpu.roll(ref[...], lax.rem(to - at + lanes, lanes), 1)
+            owned = jnp.where((lane >= to) & (lane < to + block), turned, owned)
+        out[...] = owned
+
+
+def finish_kernel(low_ref, sum_ref, mine_ref, across_ref, owned_ref, dk_ref, dv_ref):
+    owned_ref[...] = mine_ref[...] + across_ref[...]
     for part, ref in enumerate((dk_ref, dv_ref)):
         ref[...] = (sum_ref[part] + low_ref[part].astype(jnp.float32)).astype(jnp.bfloat16)
 
@@ -284,20 +301,11 @@
         dfar.reshape(subs * heads, rows, width), ("sub", "head"), 0, 0, tiled=True
     )
     down = [down[0]] + [swap(down[o], "head", o) for o in range(1, heads)]
-    natural = norm.reshape(norm.shape[0], shards, block)
-    owner = lax.dynamic_index_in_dim(block_owner, shard, 0, keepdims=False)
-    order = jnp.stack([(sub ^ d) + subs * e for e in (half, 1 - half) for d in range(subs)])
-    pick = owner[None, :] == order[:, None]
-    routed = jnp.sum(jnp.where(pick[:, None, :, None], natural[None], 0.0), axis=2)
-    routed = routed.reshape(2, subs, -1)
-    across = swap(routed[1], "half", 1)
-    ready = jnp.stack([routed[0], across], axis=1)
-    near_lse = [ready[0]] + [swap(ready[d], "sub", d) for d in range(1, subs)]
-    both = jnp.concatenate(near_lse, axis=0)
-    source = jnp.stack([(sub ^ d) + subs * e for d in range(subs) for e in (half, 1 - half)])
-    place = source[None, :] == jnp.arange(shards, dtype=jnp.int32)[:, None]
-    owned = jnp.sum(jnp.where(place[:, :, None], both[None], 0.0), axis=1)
-    owned = owned.reshape(shards, -1, block).transpose(1, 0, 2).reshape(-1, tok)
+    logs = [norm] + [swap(norm, "sub", d) for d in range(1, subs)]
+    source = half * subs + jnp.stack([sub ^ d for d in range(subs)])
+    owners = jnp.stack([shard, shard + subs - 2 * subs * half])
+    spots = jnp.argmax(block_owner[source][None] == owners[:, None, None], axis=2)
+    spots = jnp.concatenate([source, spots.reshape(-1).astype(jnp.int32)])
     low, sums = pl.pallas_call(
         functools.partial(collect_kernel, groups),
         out_shape=[
@@ -309,12 +317,21 @@
         name="collect",
     )(where, parts.reshape(subs, heads, rows, width), *down)
     low = swap(low, "half", 1)
-    dk, dv = pl.pallas_call(
+    routed = pl.pallas_call(
+        functools.partial(route_kernel, block),
+        out_shape=[jax.ShapeDtypeStruct(norm.shape, jnp.float32)] * 2,
+        in_specs=[scalar] + [vmem] * subs,
+        compiler_params=room(0),
+        name="route",
+    )(spots, *logs)
+    across = swap(routed[1], "half", 1)
+    owned, dk, dv = pl.pallas_call(
         finish_kernel,
-        out_shape=[jax.ShapeDtypeStruct(key_rows.shape, jnp.bfloat16)] * 2,
+        out_shape=[jax.ShapeDtypeStruct(norm.shape, jnp.float32)]
+        + [jax.ShapeDtypeStruct(key_rows.shape, jnp.bfloat16)] * 2,
         compiler_params=room(32 * key_rows.size),
         name="finish",
-    )(low, sums)
+    )(low, sums, routed[0], across)
     return (attention, owned, dq, dk, dv)
 
 

time: 62.1 us -> 65.4 us (1.053)
  waiting for transfers between devices: 19.2 us -> 25.8 us
  starting transfers between devices: 26.2 us -> 22.7 us
    ppermute x13, waiting for transfers between devices: 18.5 us -> 24.3 us  [swap(): lax.ppermute(x, axis, [(i, i ^ d) for i in range(lax.axis_size(axis))])]
    ppermute x13, starting transfers between devices: 18.4 us -> 15 us  [swap(): lax.ppermute(x, axis, [(i, i ^ d) for i in range(lax.axis_size(axis))])]
    all_to_all x1, waiting for transfers between devices: 0.01 us -> 0.82 us  [body(): lax.all_to_all(dfar.reshape(subs * heads, rows, width), ('sub', 'head'),...]
    another operation x1 -> x2, other arithmetic: 0.01 us -> 0.77 us  [the longest x1 0.7 us: body(): jnp.argmax(block_owner[source][None] == owners[:, None, None], axis=2)]
    reshape x2 -> x1, local copies, waits for them, and re-layouts: 0.76 us -> 0.08 us  [body(): spots = jnp.concatenate([source, spots.reshape(-1).astype(jnp.int32)])]
    pallas_call x2 -> x3, Pallas kernels: 8.33 us -> 8.47 us  [the longest x1 7.16 us: attend(): pl.pallas_call(functools.partial(attention_kernel, group, groups, len(own...]
    unnamed x16 -> x12, local copies, waits for them, and re-layouts: 2.39 us -> 2.38 us
  transfers between devices with their start and end apart: 15 -> 15, of which waited for: 8 -> 9; matrix products, arithmetic and copies ran while one was open for 3% -> 3% of each run, Pallas kernels for 2% -> 2%
where the time goes in v1:
time: 65.4 us; the launch traced here: 64.9 us
  waiting for transfers between devices  25.8 us (39%)
  starting transfers between devices  22.7 us (35%)
  Pallas kernels  11.2 us (17%)
  local copies, waits for them, and re-layouts  3.1 us (5%)
  other arithmetic  1.32 us (2%)
  between operations  0.73 us (1%)
    ppermute x13, waiting for transfers between devices, swap(): lax.ppermute(x, axis, [(i, i ^ d) for i in range(lax.axis_size(axis))])  24.3 us
    ppermute x13, starting transfers between devices, swap(): lax.ppermute(x, axis, [(i, i ^ d) for i in range(lax.axis_size(axis))])  15 us
    pallas_call x1, Pallas kernels, attend(): pl.pallas_call(functools.partial(attention_kernel, group, groups, len(own...  7.16 us
    all_to_all x1, starting transfers between devices, body(): lax.all_to_all(packed.reshape(subs * heads, rows, width), ('sub', 'head')...  4.16 us
    all_to_all x1, starting transfers between devices, body(): lax.all_to_all(dfar.reshape(subs * heads, rows, width), ('sub', 'head'),...  3.57 us
    unnamed x12, local copies, waits for them, and re-layouts  2.38 us
    pallas_call x1, Pallas kernels, body(): pl.pallas_call(functools.partial(far_kernel, groups), out_shape=jax.Shape...  1.41 us
  transfers between devices with their start and end apart: 15, of which 9 were waited for; matrix products, arithmetic and copies ran while one was open for 3% of the time, Pallas kernels for 2%

profile of v1, /device:TPU:0, one launch (start us, length us, event | category | flops | bytes accessed | tf_op | source)
XLA Modules:
  0.0 64.9 jit_solution(4753228478073744652)
XLA Ops:
  0.6 0.0 copy-start
  0.6 4.1 %collective-permute-start = (bf16[32,1024]{1,0:T(8,128)(2,1)}, bf16[32,1024]{1,0:T(8,128)(2,1)S(1)}, u32[]{:S(2)}, u32[]{:S(2)}) collective-permute-start(bf16[32,1024]{1,0:T(8,128)(2,1)} %k_ref.1), channel_id=1, source_target_pairs={{0,16},{16,0},{1,17},{17,1},{2,18},{18,2},{3,19},{19,3},{4,20},{20... | collective-permute-start | bytes 196616 | tf_op jit(solution)/shard_map/ppermute | solution.py:268
  4.8 0.1 collective-permute-start.1
  4.9 0.1 pad_add_fusion.where_ref.refs_0_
  4.9 0.0 copy-start.1
  4.9 0.8 %copy-done.1 = bf16[32,1024]{1,0:T(8,128)(2,1)S(1)} copy-done((bf16[32,1024]{1,0:T(8,128)(2,1)S(1)}, bf16[32,1024]{1,0:T(8,128)(2,1)}, u32[]{:S(2)}) %copy-start.1) | copy-done | bytes 65560
  5.8 0.0 copy-start.2
  5.8 0.8 %copy-done.2 = bf16[32,1024]{1,0:T(8,128)(2,1)S(1)} copy-done((bf16[32,1024]{1,0:T(8,128)(2,1)S(1)}, bf16[32,1024]{1,0:T(8,128)(2,1)}, u32[]{:S(2)}) %copy-start.2) | copy-done | bytes 65560
  6.6 0.6 own.1
  7.2 1.5 %collective-permute-done.kl_ref = bf16[32,1024]{1,0:T(8,128)(2,1)S(1)} collective-permute-done((bf16[32,1024]{1,0:T(8,128)(2,1)}, bf16[32,1024]{1,0:T(8,128)(2,1)S(1)}, u32[]{:S(2)}, u32[]{:S(2)}) %collective-permute-start) | collective-permute-done | bytes 65568 | tf_op jit(solution)/shard_map/ppermute | solution.py:268
  8.7 2.7 %collective-permute-done.1.vl_ref = bf16[32,1024]{1,0:T(8,128)(2,1)S(1)} collective-permute-done((bf16[32,1024]{1,0:T(8,128)(2,1)}, bf16[32,1024]{1,0:T(8,128)(2,1)S(1)}, u32[]{:S(2)}, u32[]{:S(2)}) %collective-permute-start.1) | collective-permute-done | bytes 65568 | tf_op jit(solution)/shard_map/ppermute | solution.py:268
  11.4 1.4 %far.1 = bf16[4,4,32,512]{3,2,1,0:T(8,128)(2,1)} custom-call(s32[3]{0:T(128)S(1)} %pad_add_fusion.where_ref.refs_0_, bf16[4,32,512]{2,1,0:T(8,128)(2,1)S(1)} %get-tuple-element.26.mine_ref, bf16[32,1024]{1,0:T(8,128)(2,1)S(1)} %collective-permute-done.kl_ref, bf16[32,1024]{1,0:T(8,128)(2,1)S(1)} %collective-permute-done.1.vl_ref), custom_call_target="tpu_custom_call" | custom-call | tf_op jit(solution)/shard_map/far/pallas_call | solution.py:283
  12.9 0.0 copy-start.3
  12.9 0.0 copy-start.4
  12.9 4.2 %all-to-all-start = ((bf16[16,32,512]{2,1,0:T(8,128)(2,1)}), bf16[16,32,512]{2,1,0:T(8,128)(2,1)S(1)}, u32[]{:S(2)}, u32[]{:S(2)}) async-start(bf16[16,32,512]{2,1,0:T(8,128)(2,1)} %bitcast.4), calls=%async_computation | async-start | bytes 1048576 | tf_op jit(solution)/shard_map/all_to_all | solution.py:290
  17.0 0.4 collective-permute-start.2
  17.4 1.6 %collective-permute-start.3 = (bf16[32,512]{1,0:T(8,128)(2,1)S(1)}, bf16[32,512]{1,0:T(8,128)(2,1)S(1)}, u32[]{:S(2)}, u32[]{:S(2)}) collective-permute-start(bf16[32,512]{1,0:T(8,128)(2,1)S(1)} %get-tuple-element.29), channel_id=1, source_target_pairs={{0,2},{1,3},{2,0},{3,1},{4,6},{5,7},{6,4},{7,5},{8,10},{9,11},{10,... | collective-permute-start | bytes 98312 | tf_op jit(solution)/shard_map/ppermute | solution.py:268
  19.1 0.0 collective-permute-start.4
  19.1 0.0 copy-start.5
  19.1 0.7 %copy-done.5 = s32[1024]{0:T(1024)S(1)} copy-done((s32[1024]{0:T(1024)S(1)}, s32[1024]{0:T(1024)}, u32[]{:S(2)}) %copy-start.5) | copy-done | bytes 4120
  19.8 0.1 dynamic_slice.3
  19.8 0.2 convert_reduce_fusion
  20.1 0.0 collective-permute-done.2.refs_7_
  20.1 6.7 %collective-permute-done.3.refs_8_ = bf16[32,512]{1,0:T(8,128)(2,1)S(1)} collective-permute-done((bf16[32,512]{1,0:T(8,128)(2,1)S(1)}, bf16[32,512]{1,0:T(8,128)(2,1)S(1)}, u32[]{:S(2)}, u32[]{:S(2)}) %collective-permute-start.3) | collective-permute-done | bytes 32800 | tf_op jit(solution)/shard_map/ppermute | solution.py:268
  26.8 0.0 collective-permute-done.4.refs_9_
  26.8 0.7 %all-to-all-done = bf16[16,32,512]{2,1,0:T(8,128)(2,1)S(1)} async-done(((bf16[16,32,512]{2,1,0:T(8,128)(2,1)}), bf16[16,32,512]{2,1,0:T(8,128)(2,1)S(1)}, u32[]{:S(2)}, u32[]{:S(2)}) %all-to-all-start) | async-done | bytes 524320 | tf_op jit(solution)/shard_map/all_to_all | solution.py:290
  27.6 0.0 copy-done.3
  27.6 0.0 copy-done.4
  27.6 7.2 %attend.1 = (bf16[128,2048]{1,0:T(8,128)(2,1)}, f32[16,128]{1,0:T(8,128)S(1)}, bf16[128,2048]{1,0:T(8,128)(2,1)}, bf16[4,128,512]{2,1,0:T(8,128)(2,1)}, bf16[32,...) custom-call(s32[3]{0:T(128)S(1)} %pad_add_fusion.where_ref.refs_0_, ...), custom_call_target="tpu_custom_call" | custom-call | flops 2013265920 | bytes 4194304 | tf_op jit(solution)/shard_map/attend/pallas_call | solution.py:172
  34.7 3.6 %all-to-all-start.1 = ((bf16[16,32,512]{2,1,0:T(8,128)(2,1)}), bf16[16,32,512]{2,1,0:T(8,128)(2,1)S(1)}, u32[]{:S(2)}, u32[]{:S(2)}) async-start(bf16[16,32,512]{2,1,0:T(8,128)(2,1)} %bitcast.6), calls=%async_computation.1 | async-start | bytes 1048576 | tf_op jit(solution)/shard_map/all_to_all | solution.py:300
  38.3 0.1 fusion.2
  38.4 0.0 copy-done
  38.4 0.6 gather_fusion
  39.0 0.1 pad_add_fusion.1
  39.0 0.3 collective-permute-start.5
  39.3 1.6 %collective-permute-start.6 = (bf16[32,512]{1,0:T(8,128)(2,1)S(1)}, bf16[32,512]{1,0:T(8,128)(2,1)S(1)}, u32[]{:S(2)}, u32[]{:S(2)}) collective-permute-start(bf16[32,512]{1,0:T(8,128)(2,1)S(1)} %get-tuple-element.35), channel_id=1, source_target_pairs={{0,2},{1,3},{2,0},{3,1},{4,6},{5,7},{6,4},{7,5},{8,10},{9,11},{10,... | collective-permute-start | bytes 98312 | tf_op jit(solution)/shard_map/ppermute | solution.py:268
  41.0 0.0 collective-permute-start.7
  41.0 0.7 %iota_reduce_fusion = (pred[2,4]{1,0:T(4,128)(4,1)}, s32[2,4]{1,0:T(2,128)S(1)}) fusion(s32[4,8]{1,0:T(4,128)S(1)} %gather_fusion, s32[2]{0:T(128)S(1)} %pad_add_fusion.1), kind=kLoop, calls=%fused_computation.3 | loop fusion | flops 456 | bytes 176 | tf_op jit(solution)/shard_map/body/reduce | solution.py:307
  41.7 0.0 collective-permute-done.5.refs_1_
  41.7 6.3 %collective-permute-done.6.refs_2_ = bf16[32,512]{1,0:T(8,128)(2,1)S(1)} collective-permute-done((bf16[32,512]{1,0:T(8,128)(2,1)S(1)}, bf16[32,512]{1,0:T(8,128)(2,1)S(1)}, u32[]{:S(2)}, u32[]{:S(2)}) %collective-permute-start.6) | collective-permute-done | bytes 32800 | tf_op jit(solution)/shard_map/ppermute | solution.py:268
  48.0 0.0 collective-permute-done.7.refs_3_
  48.0 0.8 %all-to-all-done.1 = bf16[16,32,512]{2,1,0:T(8,128)(2,1)S(1)} async-done(((bf16[16,32,512]{2,1,0:T(8,128)(2,1)}), bf16[16,32,512]{2,1,0:T(8,128)(2,1)S(1)}, u32[]{:S(2)}, u32[]{:S(2)}) %all-to-all-start.1) | async-done | bytes 524320 | tf_op jit(solution)/shard_map/all_to_all | solution.py:300
  48.8 0.7 %collect.1 = (bf16[2,32,1024]{2,1,0:T(8,128)(2,1)S(1)}, f32[2,32,1024]{2,1,0:T(8,128)S(1)}) custom-call(s32[3]{0:T(128)S(1)} %pad_add_fusion.where_ref.refs_0_, bf16[4,4,32,512]{3,2,1,0:T(8,128)(2,1)S(1)} %bitcast.19, bf16[32,512]{1,0:T(8,128)(2,1)S(1)} %get-tuple-element.33.refs_0_, bf16[32,512]{1,0:T(8,128)(2,1)S(1)} %collective-permute-done.5.refs_1_, ...), custom_call_target="tpu_custom_call" | custom-call | tf_op jit(solution)/shard_map/collect/pallas_call | solution.py:309
  49.5 3.2 %collective-permute-start.8 = (bf16[2,32,1024]{2,1,0:T(8,128)(2,1)S(1)}, bf16[2,32,1024]{2,1,0:T(8,128)(2,1)S(1)}, u32[]{:S(2)}, u32[]{:S(2)}) collective-permute-start(bf16[2,32,1024]{2,1,0:T(8,128)(2,1)S(1)} %get-tuple-element.37), channel_id=1, source_target_pairs={{0,16},{16,0},{1,17},{17,1},{2,18},{18,2},{3,19},{19,3},{4,20},{20... | collective-permute-start | bytes 393224 | tf_op jit(solution)/shard_map/ppermute | solution.py:268
  52.8 0.1 add_add_fusion
  52.8 0.1 reshape.101
  52.9 1.6 %collective-permute-start.11 = (f32[16,128]{1,0:T(8,128)S(1)}, f32[16,128]{1,0:T(8,128)S(1)}, u32[]{:S(2)}, u32[]{:S(2)}) collective-permute-start(f32[16,128]{1,0:T(8,128)S(1)} %get-tuple-element.40.refs_0_), channel_id=1, source_target_pairs={{0,12},{4,8},{8,4},{12,0},{1,13},{5,9},{9,5},{13,1},{2,14},{6,10},... | collective-permute-start | bytes 24584 | tf_op jit(solution)/shard_map/ppermute | solution.py:268
  54.6 0.5 collective-permute-start.10
  55.1 1.4 %collective-permute-start.9 = (f32[16,128]{1,0:T(8,128)S(1)}, f32[16,128]{1,0:T(8,128)S(1)}, u32[]{:S(2)}, u32[]{:S(2)}) collective-permute-start(f32[16,128]{1,0:T(8,128)S(1)} %get-tuple-element.40.refs_0_), channel_id=1, source_target_pairs={{0,4},{4,0},{8,12},{12,8},{1,5},{5,1},{9,13},{13,9},{2,6},{6,2},{1... | collective-permute-start | bytes 24584 | tf_op jit(solution)/shard_map/ppermute | solution.py:268
  56.4 0.1 pad_add_fusion.2.spots_ref
  56.5 1.1 %collective-permute-done.11.refs_3_ = f32[16,128]{1,0:T(8,128)S(1)} collective-permute-done((f32[16,128]{1,0:T(8,128)S(1)}, f32[16,128]{1,0:T(8,128)S(1)}, u32[]{:S(2)}, u32[]{:S(2)}) %collective-permute-start.11) | collective-permute-done | bytes 8224 | tf_op jit(solution)/shard_map/ppermute | solution.py:268
  57.5 1.4 %collective-permute-done.10.refs_2_ = f32[16,128]{1,0:T(8,128)S(1)} collective-permute-done((f32[16,128]{1,0:T(8,128)S(1)}, f32[16,128]{1,0:T(8,128)S(1)}, u32[]{:S(2)}, u32[]{:S(2)}) %collective-permute-start.10) | collective-permute-done | bytes 8224 | tf_op jit(solution)/shard_map/ppermute | solution.py:268
  59.0 0.0 collective-permute-done.9.refs_1_
  59.0 0.6 route.1
  59.6 0.1 collective-permute-start.12
  59.7 4.5 %collective-permute-done.12.across_ref = f32[16,128]{1,0:T(8,128)S(1)} collective-permute-done((f32[16,128]{1,0:T(8,128)S(1)}, f32[16,128]{1,0:T(8,128)S(1)}, u32[]{:S(2)}, u32[]{:S(2)}) %collective-permute-start.12) | collective-permute-done | bytes 8224 | tf_op jit(solution)/shard_map/ppermute | solution.py:268
  64.2 0.0 collective-permute-done.8.low_ref
  64.2 0.7 %finish.1 = (f32[16,128]{1,0:T(8,128)}, bf16[32,1024]{1,0:T(8,128)(2,1)}, bf16[32,1024]{1,0:T(8,128)(2,1)}) custom-call(bf16[2,32,1024]{2,1,0:T(8,128)(2,1)S(1)} %collective-permute-done.8.low_ref, f32[2,32,1024]{2,1,0:T(8,128)S(1)} %get-tuple-element.38.sum_ref, f32[16,128]{1,0:T(8,128)S(1)} %get-tuple-element.41.mine_ref, ...), custom_call_target="tpu_custom_call" | custom-call | tf_op jit(solution)/shard_map/finish/pallas_call | solution.py:328
  (2 shorter events, 0.0 us)
Async XLA Ops:
  0.6 37.8 %copy-start = (s32[8,8]{1,0:T(8,128)S(1)}, s32[8,8]{1,0:T(8,128)}, u32[]{:S(2)}) copy-start(s32[8,8]{1,0:T(8,128)} %param.11) | copy-start | bytes 772
  0.6 8.1 %collective-permute-start = (bf16[32,1024]{1,0:T(8,128)(2,1)}, bf16[32,1024]{1,0:T(8,128)(2,1)S(1)}, u32[]{:S(2)}, u32[]{:S(2)}) collective-permute-start(bf16[32,1024]{1,0:T(8,128)(2,1)} %k_ref.1), channel_id=1, source_target_pairs={{0,16},{16,0},{1,17},{17,1},{2,18},{18,2},{3,19},{19,3},{4,20},{20... | collective-permute-start | bytes 196616 | tf_op jit(solution)/shard_map/ppermute | solution.py:268
  4.8 6.7 %collective-permute-start.1 = (bf16[32,1024]{1,0:T(8,128)(2,1)}, bf16[32,1024]{1,0:T(8,128)(2,1)S(1)}, u32[]{:S(2)}, u32[]{:S(2)}) collective-permute-start(bf16[32,1024]{1,0:T(8,128)(2,1)} %v_ref.1), channel_id=1, source_target_pairs={{0,16},{16,0},{1,17},{17,1},{2,18},{18,2},{3,19},{19,3},{4,20},{20... | collective-permute-start | bytes 196616 | tf_op jit(solution)/shard_map/ppermute | solution.py:268
  4.9 0.8 %copy-start.1 = (bf16[32,1024]{1,0:T(8,128)(2,1)S(1)}, bf16[32,1024]{1,0:T(8,128)(2,1)}, u32[]{:S(2)}) copy-start(bf16[32,1024]{1,0:T(8,128)(2,1)} %k_ref.1) | copy-start | bytes 196612
  5.8 0.8 %copy-start.2 = (bf16[32,1024]{1,0:T(8,128)(2,1)S(1)}, bf16[32,1024]{1,0:T(8,128)(2,1)}, u32[]{:S(2)}) copy-start(bf16[32,1024]{1,0:T(8,128)(2,1)} %v_ref.1) | copy-start | bytes 196612
  12.9 14.7 %copy-start.3 = (bf16[128,2048]{1,0:T(8,128)(2,1)S(1)}, bf16[128,2048]{1,0:T(8,128)(2,1)}, u32[]{:S(2)}) copy-start(bf16[128,2048]{1,0:T(8,128)(2,1)} %refs_3_.1) | copy-start | bytes 1572868
  12.9 14.7 %copy-start.4 = (bf16[128,2048]{1,0:T(8,128)(2,1)S(1)}, bf16[128,2048]{1,0:T(8,128)(2,1)}, u32[]{:S(2)}) copy-start(bf16[128,2048]{1,0:T(8,128)(2,1)} %refs_4_.1) | copy-start | bytes 1572868
  12.9 14.7 %all-to-all-start = ((bf16[16,32,512]{2,1,0:T(8,128)(2,1)}), bf16[16,32,512]{2,1,0:T(8,128)(2,1)S(1)}, u32[]{:S(2)}, u32[]{:S(2)}) async-start(bf16[16,32,512]{2,1,0:T(8,128)(2,1)} %bitcast.4), calls=%async_computation | async-start | bytes 1048576 | tf_op jit(solution)/shard_map/all_to_all | solution.py:290
  17.0 3.0 %collective-permute-start.2 = (bf16[32,512]{1,0:T(8,128)(2,1)S(1)}, bf16[32,512]{1,0:T(8,128)(2,1)S(1)}, u32[]{:S(2)}, u32[]{:S(2)}) collective-permute-start(bf16[32,512]{1,0:T(8,128)(2,1)S(1)} %get-tuple-element.28), channel_id=1, source_target_pairs={{0,1},{1,0},{2,3},{3,2},{4,5},{5,4},{6,7},{7,6},{8,9},{9,8},{10,11... | collective-permute-start | bytes 98312 | tf_op jit(solution)/shard_map/ppermute | solution.py:268
  17.4 9.4 %collective-permute-start.3 = (bf16[32,512]{1,0:T(8,128)(2,1)S(1)}, bf16[32,512]{1,0:T(8,128)(2,1)S(1)}, u32[]{:S(2)}, u32[]{:S(2)}) collective-permute-start(bf16[32,512]{1,0:T(8,128)(2,1)S(1)} %get-tuple-element.29), channel_id=1, source_target_pairs={{0,2},{1,3},{2,0},{3,1},{4,6},{5,7},{6,4},{7,5},{8,10},{9,11},{10,... | collective-permute-start | bytes 98312 | tf_op jit(solution)/shard_map/ppermute | solution.py:268
  19.1 7.7 %collective-permute-start.4 = (bf16[32,512]{1,0:T(8,128)(2,1)S(1)}, bf16[32,512]{1,0:T(8,128)(2,1)S(1)}, u32[]{:S(2)}, u32[]{:S(2)}) collective-permute-start(bf16[32,512]{1,0:T(8,128)(2,1)S(1)} %get-tuple-element.30), channel_id=1, source_target_pairs={{0,3},{1,2},{2,1},{3,0},{4,7},{5,6},{6,5},{7,4},{8,11},{9,10},{10,... | collective-permute-start | bytes 98312 | tf_op jit(solution)/shard_map/ppermute | solution.py:268
  19.1 0.7 %copy-start.5 = (s32[1024]{0:T(1024)S(1)}, s32[1024]{0:T(1024)}, u32[]{:S(2)}) copy-start(s32[1024]{0:T(1024)} %param.10) | copy-start | bytes 12292
  34.7 14.1 %all-to-all-start.1 = ((bf16[16,32,512]{2,1,0:T(8,128)(2,1)}), bf16[16,32,512]{2,1,0:T(8,128)(2,1)S(1)}, u32[]{:S(2)}, u32[]{:S(2)}) async-start(bf16[16,32,512]{2,1,0:T(8,128)(2,1)} %bitcast.6), calls=%async_computation.1 | async-start | bytes 1048576 | tf_op jit(solution)/shard_map/all_to_all | solution.py:300
  39.0 2.6 %collective-permute-start.5 = (bf16[32,512]{1,0:T(8,128)(2,1)S(1)}, bf16[32,512]{1,0:T(8,128)(2,1)S(1)}, u32[]{:S(2)}, u32[]{:S(2)}) collective-permute-start(bf16[32,512]{1,0:T(8,128)(2,1)S(1)} %get-tuple-element.34), channel_id=1, source_target_pairs={{0,1},{1,0},{2,3},{3,2},{4,5},{5,4},{6,7},{7,6},{8,9},{9,8},{10,11... | collective-permute-start | bytes 98312 | tf_op jit(solution)/shard_map/ppermute | solution.py:268
  39.3 8.6 %collective-permute-start.6 = (bf16[32,512]{1,0:T(8,128)(2,1)S(1)}, bf16[32,512]{1,0:T(8,128)(2,1)S(1)}, u32[]{:S(2)}, u32[]{:S(2)}) collective-permute-start(bf16[32,512]{1,0:T(8,128)(2,1)S(1)} %get-tuple-element.35), channel_id=1, source_target_pairs={{0,2},{1,3},{2,0},{3,1},{4,6},{5,7},{6,4},{7,5},{8,10},{9,11},{10,... | collective-permute-start | bytes 98312 | tf_op jit(solution)/shard_map/ppermute | solution.py:268
  41.0 7.0 %collective-permute-start.7 = (bf16[32,512]{1,0:T(8,128)(2,1)S(1)}, bf16[32,512]{1,0:T(8,128)(2,1)S(1)}, u32[]{:S(2)}, u32[]{:S(2)}) collective-permute-start(bf16[32,512]{1,0:T(8,128)(2,1)S(1)} %get-tuple-element.36), channel_id=1, source_target_pairs={{0,3},{1,2},{2,1},{3,0},{4,7},{5,6},{6,5},{7,4},{8,11},{9,10},{10,... | collective-permute-start | bytes 98312 | tf_op jit(solution)/shard_map/ppermute | solution.py:268
  49.5 14.7 %collective-permute-start.8 = (bf16[2,32,1024]{2,1,0:T(8,128)(2,1)S(1)}, bf16[2,32,1024]{2,1,0:T(8,128)(2,1)S(1)}, u32[]{:S(2)}, u32[]{:S(2)}) collective-permute-start(bf16[2,32,1024]{2,1,0:T(8,128)(2,1)S(1)} %get-tuple-element.37), channel_id=1, source_target_pairs={{0,16},{16,0},{1,17},{17,1},{2,18},{18,2},{3,19},{19,3},{4,20},{20... | collective-permute-start | bytes 393224 | tf_op jit(solution)/shard_map/ppermute | solution.py:268
  52.9 4.6 %collective-permute-start.11 = (f32[16,128]{1,0:T(8,128)S(1)}, f32[16,128]{1,0:T(8,128)S(1)}, u32[]{:S(2)}, u32[]{:S(2)}) collective-permute-start(f32[16,128]{1,0:T(8,128)S(1)} %get-tuple-element.40.refs_0_), channel_id=1, source_target_pairs={{0,12},{4,8},{8,4},{12,0},{1,13},{5,9},{9,5},{13,1},{2,14},{6,10},... | collective-permute-start | bytes 24584 | tf_op jit(solution)/shard_map/ppermute | solution.py:268
  54.6 4.4 %collective-permute-start.10 = (f32[16,128]{1,0:T(8,128)S(1)}, f32[16,128]{1,0:T(8,128)S(1)}, u32[]{:S(2)}, u32[]{:S(2)}) collective-permute-start(f32[16,128]{1,0:T(8,128)S(1)} %get-tuple-element.40.refs_0_), channel_id=1, source_target_pairs={{0,8},{4,12},{8,0},{12,4},{1,9},{5,13},{9,1},{13,5},{2,10},{6,14},... | collective-permute-start | bytes 24584 | tf_op jit(solution)/shard_map/ppermute | solution.py:268
  55.1 3.9 %collective-permute-start.9 = (f32[16,128]{1,0:T(8,128)S(1)}, f32[16,128]{1,0:T(8,128)S(1)}, u32[]{:S(2)}, u32[]{:S(2)}) collective-permute-start(f32[16,128]{1,0:T(8,128)S(1)} %get-tuple-element.40.refs_0_), channel_id=1, source_target_pairs={{0,4},{4,0},{8,12},{12,8},{1,5},{5,1},{9,13},{13,9},{2,6},{6,2},{1... | collective-permute-start | bytes 24584 | tf_op jit(solution)/shard_map/ppermute | solution.py:268
  59.6 4.6 %collective-permute-start.12 = (f32[16,128]{1,0:T(8,128)S(1)}, f32[16,128]{1,0:T(8,128)S(1)}, u32[]{:S(2)}, u32[]{:S(2)}) collective-permute-start(f32[16,128]{1,0:T(8,128)S(1)} %get-tuple-element.42), channel_id=1, source_target_pairs={{0,16},{16,0},{1,17},{17,1},{2,18},{18,2},{3,19},{19,3},{4,20},{20... | collective-permute-start | bytes 24584 | tf_op jit(solution)/shard_map/ppermute | solution.py:268

commit v2 on v1

--- a/solution.py
+++ b/solution.py
@@ -29,7 +29,7 @@
     heads = mine_ref.shape[0]
     for g in range(groups):
         for part, ref in enumerate((k_ref, v_ref)):
-            to = slice((2 * g + part) * HEAD_SIZE, (2 * g + part + 1) * HEAD_SIZE)
+            to = slice((part * groups + g) * HEAD_SIZE, (part * groups + g + 1) * HEAD_SIZE)
             for h in range(heads):
                 at = (h * groups + g) * HEAD_SIZE
                 mine_ref[h, :, to] = ref[:, at : at + HEAD_SIZE]
@@ -38,35 +38,60 @@
                 own[:, to] = ref[:, pl.ds(at, HEAD_SIZE)]
 
 
-def far_kernel(groups, where_ref, mine_ref, kl_ref, vl_ref, far_ref):
+def far_kernel(groups, part, where_ref, mine_ref, low_ref, *refs):
+    far_hbm, far_ref, sem = refs[-3:]
     subs, heads = far_ref.shape[:2]
-    for g in range(groups):
-        for part, low in enumerate((kl_ref, vl_ref)):
-            to = slice((2 * g + part) * HEAD_SIZE, (2 * g + part + 1) * HEAD_SIZE)
-            for h in range(heads):
-                at = (h * groups + g) * HEAD_SIZE
-                mine = mine_ref[h, :, to]
-                theirs = low[:, at : at + HEAD_SIZE]
-                for dest in range(subs):
-                    far_ref[dest, h, :, to] = jnp.where(where_ref[1] < dest, mine, theirs)
+    cols = slice(part * groups * HEAD_SIZE, (part + 1) * groups * HEAD_SIZE)
+    for h in range(heads):
+        mine = mine_ref[h, :, cols]
+        at = h * groups * HEAD_SIZE
+        theirs = low_ref[:, at : at + groups * HEAD_SIZE]
+        for dest in range(subs):
+            far_ref[dest, h] = jnp.where(where_ref[1] < dest, mine, theirs)
+    copy = pltpu.make_async_copy(far_ref, far_hbm.at[:, :, :, cols], sem)
+    copy.start()
+    copy.wait()
 
 
 def attention_kernel(group, groups, heads, *refs):
     scratch = refs[-8 * groups :]
-    bias, refs = refs[-8 * groups - 1], refs[: -8 * groups - 1]
+    bias, o_ref, dq_ref, dfar_ref, sems = refs[-8 * groups - 5 : -8 * groups]
+    refs = list(refs[: -8 * groups - 5])
+    outs = 6 + heads
+    o_hbm, dq_hbm, dfar_hbm = refs[outs], refs[outs + 2], refs[outs + 3]
+    refs[outs], refs[outs + 2], refs[outs + 3] = o_ref, dq_ref, dfar_ref
+    copies = []
+
+    def send(src, dst):
+        copy = pltpu.make_async_copy(src, dst, sems.at[len(copies)])
+        copy.start()
+        copies.append(copy)
+
     for g in range(groups):
-        one_group(g, group, heads, bias, scratch[8 * g : 8 * g + 8], *refs)
+        wide = pl.ds(g * group * HEAD_SIZE, group * HEAD_SIZE)
+
+        def rows_done(wide=wide):
+            send(o_ref.at[:, wide], o_hbm.at[:, wide])
+            send(dq_ref.at[:, wide], dq_hbm.at[:, wide])
+
+        one_group(g, group, heads, bias, scratch[8 * g : 8 * g + 8], rows_done, *refs)
+        for part in range(2):
+            cols = pl.ds((part * groups + g) * HEAD_SIZE, HEAD_SIZE)
+            send(dfar_ref.at[:, :, cols], dfar_hbm.at[:, :, cols])
+    for copy in copies:
+        copy.wait()
 
 
 def one_group(
-    g, group, heads, bias, scratch, where_ref, base_ref, start_ref, q_ref, do_ref, far_ref, *refs
+    g, group, heads, bias, scratch, rows_done, where_ref, base_ref, start_ref, q_ref, do_ref, far_ref, *refs
 ):
     own_refs, refs = refs[:heads], refs[heads:]
     o_ref, lse_ref, dq_ref, dfar_ref = refs[:4]
     down_refs = refs[4:]
     qs, dos, kw, vw, kt, vt, p_all, ds_all = scratch
-    key_cols = slice(2 * g * HEAD_SIZE, (2 * g + 1) * HEAD_SIZE)
-    value_cols = slice((2 * g + 1) * HEAD_SIZE, (2 * g + 2) * HEAD_SIZE)
+    shift = far_ref.shape[2] // 2
+    key_cols = slice(g * HEAD_SIZE, (g + 1) * HEAD_SIZE)
+    value_cols = slice(shift + g * HEAD_SIZE, shift + (g + 1) * HEAD_SIZE)
 
     def columns(h):
         return slice((g * group + h) * HEAD_SIZE, (g * group + h + 1) * HEAD_SIZE)
@@ -149,6 +174,7 @@
             finish(*waiting.pop(0))
     while waiting:
         finish(*waiting.pop(0))
+    rows_done()
     kw[...] = (dot(ds_all[...], qs[...], NN) * scale).astype(jnp.bfloat16)
     vw[...] = dv
     for b in range(subs):
@@ -166,6 +192,7 @@
     keys = (1 + far.shape[0]) * tok
     scalar = pl.BlockSpec(memory_space=pltpu.SMEM)
     vmem = pl.BlockSpec(memory_space=pltpu.VMEM)
+    hbm = pl.BlockSpec(memory_space=pl.ANY)
     wide = jax.ShapeDtypeStruct(queries.shape, jnp.bfloat16)
     rows = group * tok
     bf = lambda *shape: pltpu.VMEM(shape, jnp.bfloat16)
@@ -179,7 +206,14 @@
         ]
         + [jax.ShapeDtypeStruct(x.shape, jnp.bfloat16) for x in own],
         in_specs=[scalar] * 2 + [vmem] * (4 + len(own)),
-        scratch_shapes=[pltpu.VMEM((keys, tok), jnp.float32)]
+        out_specs=[hbm, vmem, hbm, hbm] + [vmem] * len(own),
+        scratch_shapes=[
+            pltpu.VMEM((keys, tok), jnp.float32),
+            bf(*queries.shape),
+            bf(*queries.shape),
+            bf(*far.shape),
+            pltpu.SemaphoreType.DMA((4 * groups,)),
+        ]
         + [
             bf(rows, HEAD_SIZE),
             bf(rows, HEAD_SIZE),
@@ -209,7 +243,7 @@
     for o, ref in enumerate(own_refs):
         for g, part in pieces:
             at = pl.multiple_of(((head ^ o) * groups + g) * HEAD_SIZE, HEAD_SIZE)
-            to = (2 * g + part) * HEAD_SIZE
+            to = (part * groups + g) * HEAD_SIZE
             sum_ref[part, :, pl.ds(at, HEAD_SIZE)] = ref[
                 :, to : to + HEAD_SIZE
             ].astype(jnp.float32)
@@ -217,7 +251,7 @@
         for g, part in pieces:
             at = (h * groups + g) * HEAD_SIZE
             cols = slice(at, at + HEAD_SIZE)
-            to = (2 * g + part) * HEAD_SIZE
+            to = (part * groups + g) * HEAD_SIZE
             own = sum_ref[part, :, cols]
             low = jnp.zeros_like(own)
             for s in range(far_ref.shape[0]):
@@ -280,15 +314,26 @@
         name="own",
     )(where, key_rows, value_rows)
     own = [own[0]] + [swap(own[o], "head", o) for o in range(1, heads)]
-    packed = pl.pallas_call(
-        functools.partial(far_kernel, groups),
-        out_shape=jax.ShapeDtypeStruct((subs, heads, rows, width), jnp.bfloat16),
-        in_specs=[scalar] + [vmem] * 3,
-        compiler_params=room(8 * subs * rows * heads * width),
-        name="far",
-    )(where, mine, low_keys, low_values)
+    packed = []
+    anywhere = pl.BlockSpec(memory_space=pl.ANY)
+    for part, low in enumerate((low_keys, low_values)):
+        packed = [
+            pl.pallas_call(
+                functools.partial(far_kernel, groups, part),
+                out_shape=jax.ShapeDtypeStruct((subs, heads, rows, width), jnp.bfloat16),
+                in_specs=[scalar] + [vmem] * 2 + [anywhere] * len(packed),
+                out_specs=anywhere,
+                scratch_shapes=[
+                    pltpu.VMEM((subs, heads, rows, width // 2), jnp.bfloat16),
+                    pltpu.SemaphoreType.DMA,
+                ],
+                input_output_aliases={3: 0} if packed else {},
+                compiler_params=room(8 * subs * rows * heads * width),
+                name="far",
+            )(where, mine, low, *packed)
+        ]
     far = lax.all_to_all(
-        packed.reshape(subs * heads, rows, width), ("sub", "head"), 0, 0, tiled=True
+        packed[0].reshape(subs * heads, rows, width), ("sub", "head"), 0, 0, tiled=True
     ).reshape(subs, tok, width)
     mine = lax.dynamic_slice_in_dim(doc_ids, shard * tok, tok)
     start = jnp.sum((doc_ids[:, None] < mine[None, :]).astype(jnp.int32), axis=0, keepdims=True)

time: 65.4 us -> 65.1 us (level)
  waiting for transfers between devices: 25.8 us -> 24.6 us
  Pallas kernels: 11.2 us -> 12.1 us
    ppermute x13, waiting for transfers between devices: 24.3 us -> 23 us  [swap(): lax.ppermute(x, axis, [(i, i ^ d) for i in range(lax.axis_size(axis))])]
    pallas_call x1 -> x2, Pallas kernels: 1.41 us -> 2.55 us  [body(): pl.pallas_call(functools.partial(far_kernel, groups, part), out_shape=jax...]
  transfers between devices with their start and end apart: 15 -> 15, of which waited for: 9 -> 9; matrix products, arithmetic and copies ran while one was open for 3% -> 3% of each run, Pallas kernels for 2% -> 4%
where the time goes in v2:
time: 65.1 us; the launch traced here: 64.6 us
  waiting for transfers between devices  24.6 us (38%)
  starting transfers between devices  22.7 us (35%)
  Pallas kernels  12.1 us (19%)
  local copies, waits for them, and re-layouts  3.1 us (5%)
  other arithmetic  1.31 us (2%)
  between operations  0.77 us (1%)
    ppermute x13, waiting for transfers between devices, swap(): lax.ppermute(x, axis, [(i, i ^ d) for i in range(lax.axis_size(axis))])  23 us
    ppermute x13, starting transfers between devices, swap(): lax.ppermute(x, axis, [(i, i ^ d) for i in range(lax.axis_size(axis))])  15 us
    pallas_call x1, Pallas kernels, attend(): pl.pallas_call(functools.partial(attention_kernel, group, groups, len(own...  6.95 us
    all_to_all x1, starting transfers between devices, body(): lax.all_to_all(packed[0].reshape(subs * heads, rows, width), ('sub', 'hea...  4.18 us
    all_to_all x1, starting transfers between devices, body(): lax.all_to_all(dfar.reshape(subs * heads, rows, width), ('sub', 'head'),...  3.58 us
    pallas_call x2, Pallas kernels, body(): pl.pallas_call(functools.partial(far_kernel, groups, part), out_shape=jax...  2.55 us
    unnamed x12, local copies, waits for them, and re-layouts  2.39 us
  transfers between devices with their start and end apart: 15, of which 9 were waited for; matrix products, arithmetic and copies ran while one was open for 3% of the time, Pallas kernels for 4%

profile of v2, /device:TPU:0, one launch (start us, length us, event | category | flops | bytes accessed | tf_op | source)
XLA Modules:
  0.0 64.6 jit_solution(2826345204185722178)
XLA Ops:
  0.6 0.0 copy-start
  0.6 4.1 %collective-permute-start.1 = (bf16[32,1024]{1,0:T(8,128)(2,1)}, bf16[32,1024]{1,0:T(8,128)(2,1)S(1)}, u32[]{:S(2)}, u32[]{:S(2)}) collective-permute-start(bf16[32,1024]{1,0:T(8,128)(2,1)} %k_ref.1), channel_id=1, source_target_pairs={{0,16},{16,0},{1,17},{17,1},{2,18},{18,2},{3,19},{19,3},{4,20},{20... | collective-permute-start | bytes 196616 | tf_op jit(solution)/shard_map/ppermute | solution.py:302
  4.8 0.1 collective-permute-start
  4.9 0.1 pad_add_fusion.where_ref.refs_0_
  4.9 0.0 copy-start.1
  4.9 0.8 %copy-done.1 = bf16[32,1024]{1,0:T(8,128)(2,1)S(1)} copy-done((bf16[32,1024]{1,0:T(8,128)(2,1)S(1)}, bf16[32,1024]{1,0:T(8,128)(2,1)}, u32[]{:S(2)}) %copy-start.1) | copy-done | bytes 65560
  5.8 0.0 copy-start.2
  5.8 0.8 %copy-done.2 = bf16[32,1024]{1,0:T(8,128)(2,1)S(1)} copy-done((bf16[32,1024]{1,0:T(8,128)(2,1)S(1)}, bf16[32,1024]{1,0:T(8,128)(2,1)}, u32[]{:S(2)}) %copy-start.2) | copy-done | bytes 65560
  6.6 0.6 own.1
  7.2 1.5 %collective-permute-done.1.low_ref = bf16[32,1024]{1,0:T(8,128)(2,1)S(1)} collective-permute-done((bf16[32,1024]{1,0:T(8,128)(2,1)}, bf16[32,1024]{1,0:T(8,128)(2,1)S(1)}, u32[]{:S(2)}, u32[]{:S(2)}) %collective-permute-start.1) | collective-permute-done | bytes 65568 | tf_op jit(solution)/shard_map/ppermute | solution.py:302
  8.7 1.3 %far.2.refs_0_ = bf16[4,4,32,512]{3,2,1,0:T(8,128)(2,1)} custom-call(s32[3]{0:T(128)S(1)} %pad_add_fusion.where_ref.refs_0_, bf16[4,32,512]{2,1,0:T(8,128)(2,1)S(1)} %get-tuple-element.26.mine_ref, bf16[32,1024]{1,0:T(8,128)(2,1)S(1)} %collective-permute-done.1.low_ref), custom_call_target="tpu_custom_call" | custom-call | tf_op jit(solution)/shard_map/far/pallas_call | solution.py:321
  10.0 1.5 %collective-permute-done.low_ref = bf16[32,1024]{1,0:T(8,128)(2,1)S(1)} collective-permute-done((bf16[32,1024]{1,0:T(8,128)(2,1)}, bf16[32,1024]{1,0:T(8,128)(2,1)S(1)}, u32[]{:S(2)}, u32[]{:S(2)}) %collective-permute-start) | collective-permute-done | bytes 65568 | tf_op jit(solution)/shard_map/ppermute | solution.py:302
  11.4 1.3 %far.3 = bf16[4,4,32,512]{3,2,1,0:T(8,128)(2,1)} custom-call(s32[3]{0:T(128)S(1)} %pad_add_fusion.where_ref.refs_0_, bf16[4,32,512]{2,1,0:T(8,128)(2,1)S(1)} %get-tuple-element.26.mine_ref, bf16[32,1024]{1,0:T(8,128)(2,1)S(1)} %collective-permute-done.low_ref, bf16[4,4,32,512]{3,2,1,0:T(8,128)(2,1)} %far.2.refs_0_), custom_call_target="tpu_custom_call", output_to_operand_aliasing={{}: (3, {})} | custom-call | tf_op jit(solution)/shard_map/far/pallas_call | solution.py:321
  12.7 0.0 copy-start.3
  12.7 0.0 copy-start.4
  12.8 4.2 %all-to-all-start = ((bf16[16,32,512]{2,1,0:T(8,128)(2,1)}), bf16[16,32,512]{2,1,0:T(8,128)(2,1)S(1)}, u32[]{:S(2)}, u32[]{:S(2)}) async-start(bf16[16,32,512]{2,1,0:T(8,128)(2,1)} %bitcast.4), calls=%async_computation | async-start | bytes 1048576 | tf_op jit(solution)/shard_map/all_to_all | solution.py:335
  16.9 0.4 collective-permute-start.2
  17.3 1.6 %collective-permute-start.3 = (bf16[32,512]{1,0:T(8,128)(2,1)S(1)}, bf16[32,512]{1,0:T(8,128)(2,1)S(1)}, u32[]{:S(2)}, u32[]{:S(2)}) collective-permute-start(bf16[32,512]{1,0:T(8,128)(2,1)S(1)} %get-tuple-element.29), channel_id=1, source_target_pairs={{0,2},{1,3},{2,0},{3,1},{4,6},{5,7},{6,4},{7,5},{8,10},{9,11},{10,... | collective-permute-start | bytes 98312 | tf_op jit(solution)/shard_map/ppermute | solution.py:302
  19.0 0.0 collective-permute-start.4
  19.0 0.0 copy-start.5
  19.0 0.7 %copy-done.5 = s32[1024]{0:T(1024)S(1)} copy-done((s32[1024]{0:T(1024)S(1)}, s32[1024]{0:T(1024)}, u32[]{:S(2)}) %copy-start.5) | copy-done | bytes 4120
  19.7 0.1 dynamic_slice.3
  19.7 0.2 convert_reduce_fusion
  20.0 0.0 collective-permute-done.2.refs_7_
  20.0 6.7 %collective-permute-done.3.refs_8_ = bf16[32,512]{1,0:T(8,128)(2,1)S(1)} collective-permute-done((bf16[32,512]{1,0:T(8,128)(2,1)S(1)}, bf16[32,512]{1,0:T(8,128)(2,1)S(1)}, u32[]{:S(2)}, u32[]{:S(2)}) %collective-permute-start.3) | collective-permute-done | bytes 32800 | tf_op jit(solution)/shard_map/ppermute | solution.py:302
  26.7 0.0 collective-permute-done.4.refs_9_
  26.7 0.7 %all-to-all-done = bf16[16,32,512]{2,1,0:T(8,128)(2,1)S(1)} async-done(((bf16[16,32,512]{2,1,0:T(8,128)(2,1)}), bf16[16,32,512]{2,1,0:T(8,128)(2,1)S(1)}, u32[]{:S(2)}, u32[]{:S(2)}) %all-to-all-start) | async-done | bytes 524320 | tf_op jit(solution)/shard_map/all_to_all | solution.py:335
  27.5 0.0 copy-done.3
  27.5 0.0 copy-done.4
  27.5 6.9 %attend.1 = (bf16[128,2048]{1,0:T(8,128)(2,1)}, f32[16,128]{1,0:T(8,128)S(1)}, bf16[128,2048]{1,0:T(8,128)(2,1)}, bf16[4,128,512]{2,1,0:T(8,128)(2,1)}, bf16[32,...) custom-call(s32[3]{0:T(128)S(1)} %pad_add_fusion.where_ref.refs_0_, ...), custom_call_target="tpu_custom_call" | custom-call | flops 2013265920 | bytes 4194304 | tf_op jit(solution)/shard_map/attend/pallas_call | solution.py:199
  34.4 3.6 %all-to-all-start.1 = ((bf16[16,32,512]{2,1,0:T(8,128)(2,1)}), bf16[16,32,512]{2,1,0:T(8,128)(2,1)S(1)}, u32[]{:S(2)}, u32[]{:S(2)}) async-start(bf16[16,32,512]{2,1,0:T(8,128)(2,1)} %bitcast.6), calls=%async_computation.1 | async-start | bytes 1048576 | tf_op jit(solution)/shard_map/all_to_all | solution.py:345
  38.0 0.1 fusion.2
  38.1 0.0 copy-done
  38.1 0.6 gather_fusion
  38.7 0.1 pad_add_fusion.1
  38.8 0.3 collective-permute-start.5
  39.0 1.6 %collective-permute-start.6 = (bf16[32,512]{1,0:T(8,128)(2,1)S(1)}, bf16[32,512]{1,0:T(8,128)(2,1)S(1)}, u32[]{:S(2)}, u32[]{:S(2)}) collective-permute-start(bf16[32,512]{1,0:T(8,128)(2,1)S(1)} %get-tuple-element.35), channel_id=1, source_target_pairs={{0,2},{1,3},{2,0},{3,1},{4,6},{5,7},{6,4},{7,5},{8,10},{9,11},{10,... | collective-permute-start | bytes 98312 | tf_op jit(solution)/shard_map/ppermute | solution.py:302
  40.7 0.0 collective-permute-start.7
  40.7 0.7 %iota_reduce_fusion = (pred[2,4]{1,0:T(4,128)(4,1)}, s32[2,4]{1,0:T(2,128)S(1)}) fusion(s32[4,8]{1,0:T(4,128)S(1)} %gather_fusion, s32[2]{0:T(128)S(1)} %pad_add_fusion.1), kind=kLoop, calls=%fused_computation.3 | loop fusion | flops 456 | bytes 176 | tf_op jit(solution)/shard_map/body/reduce | solution.py:352
  41.4 0.0 collective-permute-done.5.refs_1_
  41.4 6.3 %collective-permute-done.6.refs_2_ = bf16[32,512]{1,0:T(8,128)(2,1)S(1)} collective-permute-done((bf16[32,512]{1,0:T(8,128)(2,1)S(1)}, bf16[32,512]{1,0:T(8,128)(2,1)S(1)}, u32[]{:S(2)}, u32[]{:S(2)}) %collective-permute-start.6) | collective-permute-done | bytes 32800 | tf_op jit(solution)/shard_map/ppermute | solution.py:302
  47.7 0.0 collective-permute-done.7.refs_3_
  47.7 0.8 %all-to-all-done.1 = bf16[16,32,512]{2,1,0:T(8,128)(2,1)S(1)} async-done(((bf16[16,32,512]{2,1,0:T(8,128)(2,1)}), bf16[16,32,512]{2,1,0:T(8,128)(2,1)S(1)}, u32[]{:S(2)}, u32[]{:S(2)}) %all-to-all-start.1) | async-done | bytes 524320 | tf_op jit(solution)/shard_map/all_to_all | solution.py:345
  48.5 0.7 %collect.1 = (bf16[2,32,1024]{2,1,0:T(8,128)(2,1)S(1)}, f32[2,32,1024]{2,1,0:T(8,128)S(1)}) custom-call(s32[3]{0:T(128)S(1)} %pad_add_fusion.where_ref.refs_0_, bf16[4,4,32,512]{3,2,1,0:T(8,128)(2,1)S(1)} %bitcast.19, bf16[32,512]{1,0:T(8,128)(2,1)S(1)} %get-tuple-element.33.refs_0_, bf16[32,512]{1,0:T(8,128)(2,1)S(1)} %collective-permute-done.5.refs_1_, ...), custom_call_target="tpu_custom_call" | custom-call | tf_op jit(solution)/shard_map/collect/pallas_call | solution.py:354
  49.2 3.2 %collective-permute-start.8 = (bf16[2,32,1024]{2,1,0:T(8,128)(2,1)S(1)}, bf16[2,32,1024]{2,1,0:T(8,128)(2,1)S(1)}, u32[]{:S(2)}, u32[]{:S(2)}) collective-permute-start(bf16[2,32,1024]{2,1,0:T(8,128)(2,1)S(1)} %get-tuple-element.37), channel_id=1, source_target_pairs={{0,16},{16,0},{1,17},{17,1},{2,18},{18,2},{3,19},{19,3},{4,20},{20... | collective-permute-start | bytes 393224 | tf_op jit(solution)/shard_map/ppermute | solution.py:302
  52.5 0.1 add_add_fusion
  52.6 0.1 reshape.101
  52.6 1.6 %collective-permute-start.11 = (f32[16,128]{1,0:T(8,128)S(1)}, f32[16,128]{1,0:T(8,128)S(1)}, u32[]{:S(2)}, u32[]{:S(2)}) collective-permute-start(f32[16,128]{1,0:T(8,128)S(1)} %get-tuple-element.40.refs_0_), channel_id=1, source_target_pairs={{0,12},{4,8},{8,4},{12,0},{1,13},{5,9},{9,5},{13,1},{2,14},{6,10},... | collective-permute-start | bytes 24584 | tf_op jit(solution)/shard_map/ppermute | solution.py:302
  54.3 0.5 collective-permute-start.10
  54.8 1.4 %collective-permute-start.9 = (f32[16,128]{1,0:T(8,128)S(1)}, f32[16,128]{1,0:T(8,128)S(1)}, u32[]{:S(2)}, u32[]{:S(2)}) collective-permute-start(f32[16,128]{1,0:T(8,128)S(1)} %get-tuple-element.40.refs_0_), channel_id=1, source_target_pairs={{0,4},{4,0},{8,12},{12,8},{1,5},{5,1},{9,13},{13,9},{2,6},{6,2},{1... | collective-permute-start | bytes 24584 | tf_op jit(solution)/shard_map/ppermute | solution.py:302
  56.1 0.1 pad_add_fusion.2.spots_ref
  56.2 1.1 %collective-permute-done.11.refs_3_ = f32[16,128]{1,0:T(8,128)S(1)} collective-permute-done((f32[16,128]{1,0:T(8,128)S(1)}, f32[16,128]{1,0:T(8,128)S(1)}, u32[]{:S(2)}, u32[]{:S(2)}) %collective-permute-start.11) | collective-permute-done | bytes 8224 | tf_op jit(solution)/shard_map/ppermute | solution.py:302
  57.3 1.4 %collective-permute-done.10.refs_2_ = f32[16,128]{1,0:T(8,128)S(1)} collective-permute-done((f32[16,128]{1,0:T(8,128)S(1)}, f32[16,128]{1,0:T(8,128)S(1)}, u32[]{:S(2)}, u32[]{:S(2)}) %collective-permute-start.10) | collective-permute-done | bytes 8224 | tf_op jit(solution)/shard_map/ppermute | solution.py:302
  58.7 0.0 collective-permute-done.9.refs_1_
  58.7 0.6 route.1
  59.3 0.1 collective-permute-start.12
  59.4 4.5 %collective-permute-done.12.across_ref = f32[16,128]{1,0:T(8,128)S(1)} collective-permute-done((f32[16,128]{1,0:T(8,128)S(1)}, f32[16,128]{1,0:T(8,128)S(1)}, u32[]{:S(2)}, u32[]{:S(2)}) %collective-permute-start.12) | collective-permute-done | bytes 8224 | tf_op jit(solution)/shard_map/ppermute | solution.py:302
  63.9 0.0 collective-permute-done.8.low_ref
  63.9 0.7 %finish.1 = (f32[16,128]{1,0:T(8,128)}, bf16[32,1024]{1,0:T(8,128)(2,1)}, bf16[32,1024]{1,0:T(8,128)(2,1)}) custom-call(bf16[2,32,1024]{2,1,0:T(8,128)(2,1)S(1)} %collective-permute-done.8.low_ref, f32[2,32,1024]{2,1,0:T(8,128)S(1)} %get-tuple-element.38.sum_ref, f32[16,128]{1,0:T(8,128)S(1)} %get-tuple-element.41.mine_ref, ...), custom_call_target="tpu_custom_call" | custom-call | tf_op jit(solution)/shard_map/finish/pallas_call | solution.py:373
  (2 shorter events, 0.0 us)
Async XLA Ops:
  0.6 37.5 %copy-start = (s32[8,8]{1,0:T(8,128)S(1)}, s32[8,8]{1,0:T(8,128)}, u32[]{:S(2)}) copy-start(s32[8,8]{1,0:T(8,128)} %param.11) | copy-start | bytes 772
  0.6 8.1 %collective-permute-start.1 = (bf16[32,1024]{1,0:T(8,128)(2,1)}, bf16[32,1024]{1,0:T(8,128)(2,1)S(1)}, u32[]{:S(2)}, u32[]{:S(2)}) collective-permute-start(bf16[32,1024]{1,0:T(8,128)(2,1)} %k_ref.1), channel_id=1, source_target_pairs={{0,16},{16,0},{1,17},{17,1},{2,18},{18,2},{3,19},{19,3},{4,20},{20... | collective-permute-start | bytes 196616 | tf_op jit(solution)/shard_map/ppermute | solution.py:302
  4.8 6.7 %collective-permute-start = (bf16[32,1024]{1,0:T(8,128)(2,1)}, bf16[32,1024]{1,0:T(8,128)(2,1)S(1)}, u32[]{:S(2)}, u32[]{:S(2)}) collective-permute-start(bf16[32,1024]{1,0:T(8,128)(2,1)} %v_ref.1), channel_id=1, source_target_pairs={{0,16},{16,0},{1,17},{17,1},{2,18},{18,2},{3,19},{19,3},{4,20},{20... | collective-permute-start | bytes 196616 | tf_op jit(solution)/shard_map/ppermute | solution.py:302
  4.9 0.8 %copy-start.1 = (bf16[32,1024]{1,0:T(8,128)(2,1)S(1)}, bf16[32,1024]{1,0:T(8,128)(2,1)}, u32[]{:S(2)}) copy-start(bf16[32,1024]{1,0:T(8,128)(2,1)} %k_ref.1) | copy-start | bytes 196612
  5.8 0.8 %copy-start.2 = (bf16[32,1024]{1,0:T(8,128)(2,1)S(1)}, bf16[32,1024]{1,0:T(8,128)(2,1)}, u32[]{:S(2)}) copy-start(bf16[32,1024]{1,0:T(8,128)(2,1)} %v_ref.1) | copy-start | bytes 196612
  12.7 14.7 %copy-start.3 = (bf16[128,2048]{1,0:T(8,128)(2,1)S(1)}, bf16[128,2048]{1,0:T(8,128)(2,1)}, u32[]{:S(2)}) copy-start(bf16[128,2048]{1,0:T(8,128)(2,1)} %refs_3_.1) | copy-start | bytes 1572868
  12.7 14.7 %copy-start.4 = (bf16[128,2048]{1,0:T(8,128)(2,1)S(1)}, bf16[128,2048]{1,0:T(8,128)(2,1)}, u32[]{:S(2)}) copy-start(bf16[128,2048]{1,0:T(8,128)(2,1)} %refs_4_.1) | copy-start | bytes 1572868
  12.8 14.7 %all-to-all-start = ((bf16[16,32,512]{2,1,0:T(8,128)(2,1)}), bf16[16,32,512]{2,1,0:T(8,128)(2,1)S(1)}, u32[]{:S(2)}, u32[]{:S(2)}) async-start(bf16[16,32,512]{2,1,0:T(8,128)(2,1)} %bitcast.4), calls=%async_computation | async-start | bytes 1048576 | tf_op jit(solution)/shard_map/all_to_all | solution.py:335
  16.9 3.0 %collective-permute-start.2 = (bf16[32,512]{1,0:T(8,128)(2,1)S(1)}, bf16[32,512]{1,0:T(8,128)(2,1)S(1)}, u32[]{:S(2)}, u32[]{:S(2)}) collective-permute-start(bf16[32,512]{1,0:T(8,128)(2,1)S(1)} %get-tuple-element.28), channel_id=1, source_target_pairs={{0,1},{1,0},{2,3},{3,2},{4,5},{5,4},{6,7},{7,6},{8,9},{9,8},{10,11... | collective-permute-start | bytes 98312 | tf_op jit(solution)/shard_map/ppermute | solution.py:302
  17.3 9.4 %collective-permute-start.3 = (bf16[32,512]{1,0:T(8,128)(2,1)S(1)}, bf16[32,512]{1,0:T(8,128)(2,1)S(1)}, u32[]{:S(2)}, u32[]{:S(2)}) collective-permute-start(bf16[32,512]{1,0:T(8,128)(2,1)S(1)} %get-tuple-element.29), channel_id=1, source_target_pairs={{0,2},{1,3},{2,0},{3,1},{4,6},{5,7},{6,4},{7,5},{8,10},{9,11},{10,... | collective-permute-start | bytes 98312 | tf_op jit(solution)/shard_map/ppermute | solution.py:302
  19.0 7.7 %collective-permute-start.4 = (bf16[32,512]{1,0:T(8,128)(2,1)S(1)}, bf16[32,512]{1,0:T(8,128)(2,1)S(1)}, u32[]{:S(2)}, u32[]{:S(2)}) collective-permute-start(bf16[32,512]{1,0:T(8,128)(2,1)S(1)} %get-tuple-element.30), channel_id=1, source_target_pairs={{0,3},{1,2},{2,1},{3,0},{4,7},{5,6},{6,5},{7,4},{8,11},{9,10},{10,... | collective-permute-start | bytes 98312 | tf_op jit(solution)/shard_map/ppermute | solution.py:302
  19.0 0.7 %copy-start.5 = (s32[1024]{0:T(1024)S(1)}, s32[1024]{0:T(1024)}, u32[]{:S(2)}) copy-start(s32[1024]{0:T(1024)} %param.10) | copy-start | bytes 12292
  34.4 14.1 %all-to-all-start.1 = ((bf16[16,32,512]{2,1,0:T(8,128)(2,1)}), bf16[16,32,512]{2,1,0:T(8,128)(2,1)S(1)}, u32[]{:S(2)}, u32[]{:S(2)}) async-start(bf16[16,32,512]{2,1,0:T(8,128)(2,1)} %bitcast.6), calls=%async_computation.1 | async-start | bytes 1048576 | tf_op jit(solution)/shard_map/all_to_all | solution.py:345
  38.8 2.6 %collective-permute-start.5 = (bf16[32,512]{1,0:T(8,128)(2,1)S(1)}, bf16[32,512]{1,0:T(8,128)(2,1)S(1)}, u32[]{:S(2)}, u32[]{:S(2)}) collective-permute-start(bf16[32,512]{1,0:T(8,128)(2,1)S(1)} %get-tuple-element.34), channel_id=1, source_target_pairs={{0,1},{1,0},{2,3},{3,2},{4,5},{5,4},{6,7},{7,6},{8,9},{9,8},{10,11... | collective-permute-start | bytes 98312 | tf_op jit(solution)/shard_map/ppermute | solution.py:302
  39.0 8.6 %collective-permute-start.6 = (bf16[32,512]{1,0:T(8,128)(2,1)S(1)}, bf16[32,512]{1,0:T(8,128)(2,1)S(1)}, u32[]{:S(2)}, u32[]{:S(2)}) collective-permute-start(bf16[32,512]{1,0:T(8,128)(2,1)S(1)} %get-tuple-element.35), channel_id=1, source_target_pairs={{0,2},{1,3},{2,0},{3,1},{4,6},{5,7},{6,4},{7,5},{8,10},{9,11},{10,... | collective-permute-start | bytes 98312 | tf_op jit(solution)/shard_map/ppermute | solution.py:302
  40.7 7.0 %collective-permute-start.7 = (bf16[32,512]{1,0:T(8,128)(2,1)S(1)}, bf16[32,512]{1,0:T(8,128)(2,1)S(1)}, u32[]{:S(2)}, u32[]{:S(2)}) collective-permute-start(bf16[32,512]{1,0:T(8,128)(2,1)S(1)} %get-tuple-element.36), channel_id=1, source_target_pairs={{0,3},{1,2},{2,1},{3,0},{4,7},{5,6},{6,5},{7,4},{8,11},{9,10},{10,... | collective-permute-start | bytes 98312 | tf_op jit(solution)/shard_map/ppermute | solution.py:302
  49.2 14.7 %collective-permute-start.8 = (bf16[2,32,1024]{2,1,0:T(8,128)(2,1)S(1)}, bf16[2,32,1024]{2,1,0:T(8,128)(2,1)S(1)}, u32[]{:S(2)}, u32[]{:S(2)}) collective-permute-start(bf16[2,32,1024]{2,1,0:T(8,128)(2,1)S(1)} %get-tuple-element.37), channel_id=1, source_target_pairs={{0,16},{16,0},{1,17},{17,1},{2,18},{18,2},{3,19},{19,3},{4,20},{20... | collective-permute-start | bytes 393224 | tf_op jit(solution)/shard_map/ppermute | solution.py:302
  52.6 4.6 %collective-permute-start.11 = (f32[16,128]{1,0:T(8,128)S(1)}, f32[16,128]{1,0:T(8,128)S(1)}, u32[]{:S(2)}, u32[]{:S(2)}) collective-permute-start(f32[16,128]{1,0:T(8,128)S(1)} %get-tuple-element.40.refs_0_), channel_id=1, source_target_pairs={{0,12},{4,8},{8,4},{12,0},{1,13},{5,9},{9,5},{13,1},{2,14},{6,10},... | collective-permute-start | bytes 24584 | tf_op jit(solution)/shard_map/ppermute | solution.py:302
  54.3 4.4 %collective-permute-start.10 = (f32[16,128]{1,0:T(8,128)S(1)}, f32[16,128]{1,0:T(8,128)S(1)}, u32[]{:S(2)}, u32[]{:S(2)}) collective-permute-start(f32[16,128]{1,0:T(8,128)S(1)} %get-tuple-element.40.refs_0_), channel_id=1, source_target_pairs={{0,8},{4,12},{8,0},{12,4},{1,9},{5,13},{9,1},{13,5},{2,10},{6,14},... | collective-permute-start | bytes 24584 | tf_op jit(solution)/shard_map/ppermute | solution.py:302
  54.8 3.9 %collective-permute-start.9 = (f32[16,128]{1,0:T(8,128)S(1)}, f32[16,128]{1,0:T(8,128)S(1)}, u32[]{:S(2)}, u32[]{:S(2)}) collective-permute-start(f32[16,128]{1,0:T(8,128)S(1)} %get-tuple-element.40.refs_0_), channel_id=1, source_target_pairs={{0,4},{4,0},{8,12},{12,8},{1,5},{5,1},{9,13},{13,9},{2,6},{6,2},{1... | collective-permute-start | bytes 24584 | tf_op jit(solution)/shard_map/ppermute | solution.py:302
  59.3 4.6 %collective-permute-start.12 = (f32[16,128]{1,0:T(8,128)S(1)}, f32[16,128]{1,0:T(8,128)S(1)}, u32[]{:S(2)}, u32[]{:S(2)}) collective-permute-start(f32[16,128]{1,0:T(8,128)S(1)} %get-tuple-element.42), channel_id=1, source_target_pairs={{0,16},{16,0},{1,17},{17,1},{2,18},{18,2},{3,19},{19,3},{4,20},{20... | collective-permute-start | bytes 24584 | tf_op jit(solution)/shard_map/ppermute | solution.py:302
